TPU v7x, 256 devices: a whole 4x4x8 slice. The times are simulated.
256 devices in a mesh: section: 4 (over y), gy: 8 (over z), gx: 8 (over x, core).
Axes of the slice: x: 4, y: 4, z: 8, core: 2. Of those that a mesh axis runs over, the one named last changes fastest.
Arguments:
- level_input: bfloat16 [4, 4, 64, 128, 320], P('section', None, 'gy', 'gx'), may hold values from -72 to 72, as said below
- out_grad: bfloat16 [4, 4, 64, 128, 320], P('section', None, 'gy', 'gx'), may hold values from -6 to 6
- conv_weight: bfloat16 [4, 27, 320, 320], P('section'), may hold values from -0.0625 to 0.0625
- norm_gain: float32 [4, 320], P('section'), may hold values from 0.1 to 1.9
- norm_shift: float32 [4, 320], P('section'), may hold values from -3 to 3
Outputs:
- upstream_grad: bfloat16 [4, 4, 64, 128, 320], P('section', None, 'gy', 'gx')
- weight_grad: float32 [4, 8640, 320], P('section', ('gy', 'gx'))
- param_grad: float32 [4, 3, 320], P('section')
Inputs may be any that keep to these rules, and one draw needn't show every extreme that they name: `level_input`: level input values of order one with varying channel and position scales.
All inputs are finite; a program needn't handle non-finite values.
Results may differ from a plain program's by a relative error of at most 0.0029.
Values may be sent and summed in bfloat16 or wider, within the bound.
A program may use at most 128 MiB of HBM per device.

v0:
```python
import jax
import jax.numpy as jnp
from jax import lax
from jax.sharding import PartitionSpec as P

G = 32


eps = 1e-05


def from_everyone(shard, axis):
    count = lax.axis_size(axis)
    return lax.all_to_all(
        jnp.broadcast_to(shard[None], (count, *shard.shape)), axis, 0, 0, tiled=True
    )


def taken_together(shard, axis):
    everything = from_everyone(shard, axis)
    return jnp.sum(everything, axis=0)


def packed_total(arrays, axis):
    line, at, done = (jnp.concatenate([a.reshape(-1) for a in arrays]), 0, [])
    subtotal = taken_together(line, axis)
    for a in arrays:
        done.append(subtotal[at : at + a.size].reshape(a.shape))
        at += a.size
    return tuple(done)


def padded(block, sides, width):
    for axis, dim in sides:
        count = lax.axis_size(axis)
        forward = [(i, i + 1) for i in range(count - 1)]
        backward = [(target, source) for source, target in forward]
        low = lax.ppermute(
            lax.slice_in_dim(block, block.shape[dim] - width, None, axis=dim), axis, forward
        )
        high = lax.ppermute(lax.slice_in_dim(block, 0, width, axis=dim), axis, backward)
        block = jnp.concatenate([low, block, high], axis=dim)
    return block


def in_one(arrays, axis):
    ends = [0]
    for a in arrays:
        ends.append(ends[-1] + a.size)
    subtotal = lax.psum(jnp.concatenate([a.ravel() for a in arrays]), axis)
    return tuple((subtotal[b:e].reshape(a.shape) for a, b, e in zip(arrays, ends, ends[1:])))


def passed_along(shard, axis, by):
    count = lax.axis_size(axis)
    pairs = [(i, i + by) for i in range(count) if 0 <= i + by < count]
    return lax.ppermute(shard, axis, pairs)


def expand_groups(values, groups, per_group):
    return jnp.broadcast_to(values[:, None], (groups, per_group)).reshape(groups * per_group)


def local(level_input, out_grad, conv_weight, norm_gain, norm_shift):
    level_x = level_input[0]
    grad_cells = out_grad[0]
    kernel_all = conv_weight[0]
    gain_vec = norm_gain[0]
    shift_vec = norm_shift[0]
    frames, rows_h, cols_w, channels = level_x.shape
    groups = G
    per_group = channels // groups
    cell_count = frames * rows_h * cols_w
    members = cell_count * per_group * lax.axis_size("gy") * lax.axis_size("gx")
    x_float = level_x.astype(jnp.float32).reshape(cell_count, groups, per_group)
    sum_first, sum_second = packed_total(
        (jnp.sum(x_float, axis=(0, 2)), jnp.sum(x_float * x_float, axis=(0, 2))), ("gy", "gx")
    )
    group_mean = sum_first / members
    group_var = sum_second / members - group_mean * group_mean
    centered = x_float - group_mean[None, :, None]
    inv_std = 1.0 / jnp.sqrt(group_var + eps)
    normed = (centered * inv_std[None, :, None]).reshape(cell_count, channels)
    activ = normed * gain_vec[None, :] + shift_vec[None, :]
    sigmoid_v = jax.nn.sigmoid(activ)
    unit_rows = (activ * sigmoid_v).astype(jnp.bfloat16)
    extended = padded(grad_cells, (("gy", 1), ("gx", 2)), 1)
    framed = jnp.pad(extended, ((1, 1), (0, 0), (0, 0), (0, 0)))
    weight_pieces = []
    input_side = jnp.zeros((cell_count, channels), jnp.float32)
    for offset_f in range(3):
        for offset_h in range(3):
            for offset_w in range(3):
                kernel_idx = offset_f * 9 + offset_h * 3 + offset_w
                window = framed[
                    2 - offset_f : 2 - offset_f + frames,
                    2 - offset_h : 2 - offset_h + rows_h,
                    2 - offset_w : 2 - offset_w + cols_w,
                    :,
                ].reshape(cell_count, channels)
                input_side = input_side + lax.dot_general(
                    window,
                    kernel_all[kernel_idx],
                    (((1,), (1,)), ((), ())),
                    preferred_element_type=jnp.float32,
                )
                weight_pieces.append(
                    lax.dot_general(
                        unit_rows,
                        window,
                        (((0,), (0,)), ((), ())),
                        preferred_element_type=jnp.float32,
                    )
                )
    weight_part = lax.psum_scatter(
        jnp.concatenate(weight_pieces, axis=0), ("gy", "gx"), scatter_dimension=0, tiled=True
    )
    silu_slope = sigmoid_v * (1.0 + activ * (1.0 - sigmoid_v))
    act_grad = input_side * silu_slope
    grad_float = grad_cells.astype(jnp.float32).reshape(cell_count, channels)
    gain_sum, shift_sum, bias_sum = in_one(
        (
            jnp.sum(act_grad * normed, axis=0),
            jnp.sum(act_grad, axis=0),
            jnp.sum(grad_float, axis=0),
        ),
        ("gy", "gx"),
    )
    mean_first = jnp.sum((gain_vec * shift_sum).reshape(groups, per_group), axis=1) / members
    mean_second = jnp.sum((gain_vec * gain_sum).reshape(groups, per_group), axis=1) / members
    norm_grad = (
        act_grad * gain_vec[None, :]
        - expand_groups(mean_first, groups, per_group)[None, :]
        - normed * expand_groups(mean_second, groups, per_group)[None, :]
    ) * expand_groups(inv_std, groups, per_group)[None, :]
    level_grad = (
        (grad_float + norm_grad).astype(jnp.bfloat16).reshape(1, frames, rows_h, cols_w, channels)
    )
    upstream_grad = passed_along(level_grad, "section", -1)
    param_grad = jnp.stack([gain_sum, shift_sum, bias_sum])[None]
    return (upstream_grad, weight_part[None], param_grad)


def solution(mesh):
    return jax.shard_map(
        local,
        mesh=mesh,
        in_specs=(
            P("section", None, "gy", "gx", None),
            P("section", None, "gy", "gx", None),
            P("section", None, None, None),
            P("section", None),
            P("section", None),
        ),
        out_specs=(
            P("section", None, "gy", "gx", None),
            P("section", ("gy", "gx"), None),
            P("section", None, None),
        ),
        check_vma=False,
    )
```

profile of v0, /device:TPU:8, one launch (start us, length us, event | category | flops | bytes accessed | tf_op | source)
XLA Modules:
  0.0 333.7 jit_solution(14471769354519032061)
XLA Ops:
  9.5 11.9 %all-to-all-start = ((f32[64,1,64]{2,1,0:T(1,128)}), f32[64,1,64]{2,1,0:T(1,128)S(1)}, u32[]{:S(2)}, u32[]{:S(2)}) async-start(f32[64,1,64]{2,1,0:T(1,128)} %broadcast_in_dim.10), calls=%async_computation | async-start | bytes 65536 | tf_op jit(solution)/shard_map/all_to_all | solution.py:14
  23.7 4.5 %collective-permute-start = (bf16[4,1,16,320]{3,2,1,0:T(8,128)(2,1)S(1)}, bf16[4,1,16,320]{3,2,1,0:T(8,128)(2,1)S(1)}, u32[]{:S(2)}, u32[]{:S(2)}) collective-permute-start(bf16[4,1,16,320]{3,2,1,0:T(8,128)(2,1)S(1)} %get-tuple-element.54), channel_id=1, source_target_pairs={{0,8},{8,16},{16,24},{24,32},{32,40},{40,48},{48,56},{1,9},{9,17},... | collective-permute-start | bytes 122888 | tf_op jit(solution)/shard_map/ppermute | solution.py:38
  28.2 1.7 convert_reduce_fusion
  29.9 2.0 copy.26
  33.3 1.9 copy.24
  37.1 2.2 convolution_bitcast_fusion
  41.8 3.0 collective-permute-start.2
  49.0 1.9 fusion.68
  54.1 2.5 fusion.26
  59.0 1.3 convolution_add_fusion.23
  78.8 2.2 convolution_add_fusion.15
  96.4 14.0 %concatenate.39 = f32[8640,320]{0,1:T(8,128)} concatenate(f32[320,320]{0,1:T(8,128)} %fusion.73, f32[320,320]{0,1:T(8,128)} %fusion.74, f32[320,320]{0,1:T(8,128)} %fusion.75, f32[320,320]{0,1:T(8,128)} %fusion.76, f32[320,320]{0,1:T(8,128)} %fusion.77, f32[320,320]{0,1:T(8,128)} %fusion.78, f32[320,320]{0,1:T(8,128)} %fusion.79, f32[320,320]{0,1:T(8,128)} %fusion.80, ...), dimensions={0} | concatenate | bytes 22118400 | tf_op jit(solution)/shard_map/concatenate | solution.py:116
  110.5 2.0 fusion.3
  112.5 1.4 fusion.19
  113.9 1.4 convolution_add_fusion.13
  115.4 1.3 convolution_add_fusion.12
  116.7 1.3 convolution_add_fusion.11
  118.0 1.3 convolution_add_fusion.10
  119.3 1.3 fusion.2
  120.7 1.3 convolution_add_fusion.8
  122.0 1.4 convolution_add_fusion.7
  123.5 1.3 convolution_add_fusion.6
  124.8 1.3 convolution_add_fusion.5
  126.1 1.4 convolution_add_fusion.4
  127.5 1.3 convolution_add_fusion.3
  128.9 1.3 convolution_add_fusion.2
  130.2 1.3 convolution_add_fusion.1
  131.6 1.6 multiply_reduce_fusion.1
  133.3 127.8 %psum.7 = f32[960]{0:T(1024)S(1)} all-reduce(f32[960]{0:T(1024)S(1)} %pad_maximum_fusion.7), channel_id=1, replica_groups=mesh['section'=4,'gy'=8,'gx'=8] {'gy','gx'}, use_global_device_ids=true, to_apply=%region_8.9 | all-reduce | flops 960 | bytes 7680 | tf_op jit(solution)/shard_map/psum | solution.py:50
  262.4 2.4 collective-permute-start.4
  266.7 5.4 %collective-permute-done.4 = bf16[1,4,8,16,320]{4,3,2,1,0:T(8,128)(2,1)S(1)} collective-permute-done((bf16[1,4,8,16,320]{4,3,2,1,0:T(8,128)(2,1)S(1)}, bf16[1,4,8,16,320]{4,3,2,1,0:T(8,128)(2,1)S(1)}, u32[]{:S(2)}, u32[]{:S(2)}) %collective-permute-start.4) | collective-permute-done | bytes 327712 | tf_op jit(solution)/shard_map/ppermute | solution.py:57
  272.1 52.0 %all-reduce.4.cloned.1.call-done = f32[8640,320]{0,1:T(8,128)} async-done(((f32[8640,320]{0,1:T(8,128)}), f32[8640,320]{0,1:T(8,128)}) %all-reduce.4.cloned.1.call-update) | async-done | bytes 11059216
  (146 shorter events, 59.2 us)
Async XLA Ops:
  7.2 41.4 %copy-start = (bf16[1,4,8,16,320]{4,3,2,1,0:T(8,128)(2,1)S(1)}, bf16[1,4,8,16,320]{4,3,2,1,0:T(8,128)(2,1)}, u32[]{:S(2)}) copy-start(bf16[1,4,8,16,320]{4,3,2,1,0:T(8,128)(2,1)} %param.6) | copy-start | bytes 983044
  9.5 25.8 %all-to-all-start = ((f32[64,1,64]{2,1,0:T(1,128)}), f32[64,1,64]{2,1,0:T(1,128)S(1)}, u32[]{:S(2)}, u32[]{:S(2)}) async-start(f32[64,1,64]{2,1,0:T(1,128)} %broadcast_in_dim.10), calls=%async_computation | async-start | bytes 65536 | tf_op jit(solution)/shard_map/all_to_all | solution.py:14
  21.5 302.6 %all-reduce.4.cloned.1.call-start = ((), (), s32[]{:S(2)}) async-start(), calls=%async_computation.1 | async-start | bytes 22282240
  22.4 16.9 %collective-permute-start.1 = (bf16[4,1,16,320]{3,2,1,0:T(8,128)(2,1)S(1)}, bf16[4,1,16,320]{3,2,1,0:T(8,128)(2,1)S(1)}, u32[]{:S(2)}, u32[]{:S(2)}) collective-permute-start(bf16[4,1,16,320]{3,2,1,0:T(8,128)(2,1)S(1)} %get-tuple-element.55), channel_id=1, source_target_pairs={{8,0},{16,8},{24,16},{32,24},{40,32},{48,40},{56,48},{9,1},{17,9},... | collective-permute-start | bytes 122888 | tf_op jit(solution)/shard_map/ppermute | solution.py:41
  23.7 15.6 %collective-permute-start = (bf16[4,1,16,320]{3,2,1,0:T(8,128)(2,1)S(1)}, bf16[4,1,16,320]{3,2,1,0:T(8,128)(2,1)S(1)}, u32[]{:S(2)}, u32[]{:S(2)}) collective-permute-start(bf16[4,1,16,320]{3,2,1,0:T(8,128)(2,1)S(1)} %get-tuple-element.54), channel_id=1, source_target_pairs={{0,8},{8,16},{16,24},{24,32},{32,40},{40,48},{48,56},{1,9},{9,17},... | collective-permute-start | bytes 122888 | tf_op jit(solution)/shard_map/ppermute | solution.py:38
  32.6 9.2 %copy-start.26 = (f32[320]{0:T(512)}, f32[320]{0:T(512)S(1)}, u32[]{:S(2)}) copy-start(f32[320]{0:T(512)S(1)} %reduce.7) | copy-start | bytes 3844
  33.3 8.5 %copy-start.19 = (f32[320]{0:T(512)}, f32[320]{0:T(512)S(1)}, u32[]{:S(2)}) copy-start(f32[320]{0:T(512)S(1)} %reduce.6) | copy-start | bytes 3844
  35.6 6.2 %copy-start.21 = (f32[320]{0:T(512)}, f32[320]{0:T(512)S(1)}, u32[]{:S(2)}) copy-start(f32[320]{0:T(512)S(1)} %mul.173) | copy-start | bytes 3844
  35.8 6.0 %copy-start.23 = (f32[320]{0:T(512)}, f32[320]{0:T(512)S(1)}, u32[]{:S(2)}) copy-start(f32[320]{0:T(512)S(1)} %sub.64) | copy-start | bytes 3844
  39.3 9.2 %copy-start.15 = (bf16[4,1,16,320]{3,2,1,0:T(8,128)(2,1)}, bf16[4,1,16,320]{3,2,1,0:T(8,128)(2,1)S(1)}, u32[]{:S(2)}) copy-start(bf16[4,1,16,320]{3,2,1,0:T(8,128)(2,1)S(1)} %collective-permute-done.1) | copy-start | bytes 122884
  39.3 9.2 %copy-start.17 = (bf16[4,1,16,320]{3,2,1,0:T(8,128)(2,1)}, bf16[4,1,16,320]{3,2,1,0:T(8,128)(2,1)S(1)}, u32[]{:S(2)}) copy-start(bf16[4,1,16,320]{3,2,1,0:T(8,128)(2,1)S(1)} %collective-permute-done) | copy-start | bytes 122884
  40.5 8.0 %collective-permute-start.3 = (bf16[4,10,1,320]{3,2,1,0:T(2,128)(2,1)S(1)}, bf16[4,10,1,320]{3,2,1,0:T(2,128)(2,1)S(1)}, u32[]{:S(2)}, u32[]{:S(2)}) collective-permute-start(bf16[4,10,1,320]{3,2,1,0:T(2,128)(2,1)S(1)} %get-tuple-element.50), channel_id=1, source_target_pairs={{1,0},{2,1},{3,2},{4,3},{5,4},{6,5},{7,6},{9,8},{10,9},{11,10},{12... | collective-permute-start | bytes 76808 | tf_op jit(solution)/shard_map/ppermute | solution.py:41
  41.8 6.7 %collective-permute-start.2 = (bf16[4,10,1,320]{3,2,1,0:T(2,128)(2,1)S(1)}, bf16[4,10,1,320]{3,2,1,0:T(2,128)(2,1)S(1)}, u32[]{:S(2)}, u32[]{:S(2)}) collective-permute-start(bf16[4,10,1,320]{3,2,1,0:T(2,128)(2,1)S(1)} %get-tuple-element.51), channel_id=1, source_target_pairs={{0,1},{1,2},{2,3},{3,4},{4,5},{5,6},{6,7},{8,9},{9,10},{10,11},{11... | collective-permute-start | bytes 76808 | tf_op jit(solution)/shard_map/ppermute | solution.py:38
  50.9 44.3 %copy-start.12 = (bf16[4,8,16,320]{3,2,1,0:T(8,128)(2,1)}, bf16[4,8,16,320]{3,2,1,0:T(8,128)(2,1)S(1)}, u32[]{:S(2)}) copy-start(bf16[4,8,16,320]{3,2,1,0:T(8,128)(2,1)S(1)} %get-tuple-element.24) | copy-start | bytes 983044
  54.1 26.9 %copy-start.9 = (bf16[4,8,16,320]{3,2,1,0:T(8,128)(2,1)}, bf16[4,8,16,320]{3,2,1,0:T(8,128)(2,1)S(1)}, u32[]{:S(2)}) copy-start(bf16[4,8,16,320]{3,2,1,0:T(8,128)(2,1)S(1)} %get-tuple-element.43) | copy-start | bytes 983044
  54.1 28.1 %copy-start.7 = (bf16[4,8,16,320]{3,2,1,0:T(8,128)(2,1)}, bf16[4,8,16,320]{3,2,1,0:T(8,128)(2,1)S(1)}, u32[]{:S(2)}) copy-start(bf16[4,8,16,320]{3,2,1,0:T(8,128)(2,1)S(1)} %get-tuple-element.64) | copy-start | bytes 983044
  54.1 29.3 %copy-start.5 = (bf16[4,8,16,320]{3,2,1,0:T(8,128)(2,1)}, bf16[4,8,16,320]{3,2,1,0:T(8,128)(2,1)S(1)}, u32[]{:S(2)}) copy-start(bf16[4,8,16,320]{3,2,1,0:T(8,128)(2,1)S(1)} %get-tuple-element.42) | copy-start | bytes 983044
  54.1 30.4 %copy-start.4 = (bf16[4,8,16,320]{3,2,1,0:T(8,128)(2,1)}, bf16[4,8,16,320]{3,2,1,0:T(8,128)(2,1)S(1)}, u32[]{:S(2)}) copy-start(bf16[4,8,16,320]{3,2,1,0:T(8,128)(2,1)S(1)} %get-tuple-element.63) | copy-start | bytes 983044
  110.5 6.2 %copy-start.8 = (bf16[4,8,16,320]{3,2,1,0:T(8,128)(2,1)S(1)}, bf16[4,8,16,320]{3,2,1,0:T(8,128)(2,1)}, u32[]{:S(2)}) copy-start(bf16[4,8,16,320]{3,2,1,0:T(8,128)(2,1)} %copy-done.7) | copy-start | bytes 983044
  110.5 7.5 %copy-start.6 = (bf16[4,8,16,320]{3,2,1,0:T(8,128)(2,1)S(1)}, bf16[4,8,16,320]{3,2,1,0:T(8,128)(2,1)}, u32[]{:S(2)}) copy-start(bf16[4,8,16,320]{3,2,1,0:T(8,128)(2,1)} %copy-done.5) | copy-start | bytes 983044
  110.5 8.8 %copy-start.2 = (bf16[4,8,16,320]{3,2,1,0:T(8,128)(2,1)S(1)}, bf16[4,8,16,320]{3,2,1,0:T(8,128)(2,1)}, u32[]{:S(2)}) copy-start(bf16[4,8,16,320]{3,2,1,0:T(8,128)(2,1)} %copy-done.1) | copy-start | bytes 983044
  122.0 9.6 %copy-start.10 = (f32[512,320]{0,1:T(8,128)S(1)}, f32[512,320]{0,1:T(8,128)}, u32[]{:S(2)}) copy-start(f32[512,320]{0,1:T(8,128)} %copy.26) | copy-start | bytes 1966084
  122.0 9.6 %copy-start.13 = (bf16[4,8,16,320]{3,2,1,0:T(8,128)(2,1)S(1)}, bf16[4,8,16,320]{3,2,1,0:T(8,128)(2,1)}, u32[]{:S(2)}) copy-start(bf16[4,8,16,320]{3,2,1,0:T(8,128)(2,1)} %copy-done.12) | copy-start | bytes 983044
  122.0 9.6 %copy-start.20 = (f32[320]{0:T(512)S(1)}, f32[320]{0:T(512)}, u32[]{:S(2)}) copy-start(f32[320]{0:T(512)} %copy-done.19) | copy-start | bytes 3844
  122.0 9.6 %copy-start.22 = (f32[320]{0:T(512)S(1)}, f32[320]{0:T(512)}, u32[]{:S(2)}) copy-start(f32[320]{0:T(512)} %copy-done.21) | copy-start | bytes 3844
  122.0 9.6 %copy-start.24 = (f32[320]{0:T(512)S(1)}, f32[320]{0:T(512)}, u32[]{:S(2)}) copy-start(f32[320]{0:T(512)} %copy-done.23) | copy-start | bytes 3844
  122.0 9.6 %copy-start.27 = (f32[320]{0:T(512)S(1)}, f32[320]{0:T(512)}, u32[]{:S(2)}) copy-start(f32[320]{0:T(512)} %copy-done.26) | copy-start | bytes 3844
  126.1 7.1 %copy-start.25 = (f32[320]{0:T(512)S(1)}, f32[320]{0:T(512)}, u32[]{:S(2)}) copy-start(f32[320]{0:T(512)} %convert_reduce_fusion) | copy-start | bytes 3844
  126.1 135.8 %copy-start.11 = (f32[512,320]{0,1:T(8,128)S(1)}, f32[512,320]{0,1:T(8,128)}, u32[]{:S(2)}) copy-start(f32[512,320]{0,1:T(8,128)} %copy.26) | copy-start | bytes 1966084
  126.1 135.8 %copy-start.14 = (bf16[512,320]{0,1:T(8,128)(2,1)S(1)}, bf16[512,320]{0,1:T(8,128)(2,1)}, u32[]{:S(2)}) copy-start(bf16[512,320]{0,1:T(8,128)(2,1)} %copy.24) | copy-start | bytes 983044
  128.9 136.0 %copy-start.28 = (u32[256]{0:T(256)S(1)}, u32[256]{0:T(256)}, u32[]{:S(2)}) copy-start(u32[256]{0:T(256)} %constant.25) | copy-start | bytes 3076
  262.4 9.7 %collective-permute-start.4 = (bf16[1,4,8,16,320]{4,3,2,1,0:T(8,128)(2,1)S(1)}, bf16[1,4,8,16,320]{4,3,2,1,0:T(8,128)(2,1)S(1)}, u32[]{:S(2)}, u32[]{:S(2)}) collective-permute-start(bf16[1,4,8,16,320]{4,3,2,1,0:T(8,128)(2,1)S(1)} %bitcast.295), channel_id=1, source_target_pairs={{64,0},{128,64},{192,128},{65,1},{129,65},{193,129},{66,2},{130,66... | collective-permute-start | bytes 983048 | tf_op jit(solution)/shard_map/ppermute | solution.py:57
  (4 other events, 13.6 us)
Sparse Core Ops, SparseCore 0:
  110.6 213.4 all-reduce.3
where the time goes:
time: 337 us; the launch traced here: 334 us
  blocking collectives  128 us (38%)
  matrix products  71.6 us (21%)
  waiting for transfers between devices  57.4 us (17%)
  local copies, waits for them, and re-layouts  27.1 us (8%)
  starting transfers between devices  24.5 us (7%)
  between operations  15.5 us (5%)
  other arithmetic  9.78 us (3%)
    psum x1, blocking collectives, in_one(): subtotal = lax.psum(jnp.concatenate([a.ravel() for a in arrays]), axis)  128 us
    unnamed x2, waiting for transfers between devices  52 us
    dot_general x27, matrix products, local(): lax.dot_general(window, kernel_all[kernel_idx], (((1,), (1,)), ((), ())),...  38.7 us
    dot_general x27, matrix products, local(): lax.dot_general(unit_rows, window, (((0,), (0,)), ((), ())), preferred_el...  32.9 us
    concatenate x1, local copies, waits for them, and re-layouts, local(): jnp.concatenate(weight_pieces, axis=0)  14 us
    all_to_all x1, starting transfers between devices, from_everyone(): lax.all_to_all(jnp.broadcast_to(shard[None], (count, *shard.shape)), axis...  11.9 us
    ppermute x2, starting transfers between devices, padded(): lax.ppermute(lax.slice_in_dim(block, block.shape[dim] - width, None, axis...  7.58 us
  transfers between devices with their start and end apart: 7, of which 2 were waited for; matrix products, arithmetic and copies ran while one was open for 12% of the time, Pallas kernels for 0%

commit v1 on v0

v1 whole, which is shorter than its diff:
```python
import functools

import jax
import jax.numpy as jnp
from jax import lax
from jax.experimental import pallas as pl
from jax.experimental.pallas import tpu as pltpu
from jax.sharding import PartitionSpec as P

G = 32
EPS = 1e-05
MESH = pl.DeviceIdType.MESH
SUB = 5
SLAB = 1080
ROWS = SLAB // SUB
F32 = jnp.float32
BF16 = jnp.bfloat16


def kernel(x_ref, g_ref, w_hbm, gain_ref, shift_ref, grp_ref,
           up_ref, dw_ref, par_ref,
           wbuf, gs, pgs, gf, tmp, edge_out, edge_l, edge_r,
           st_x, rx_sx, st_z, rx_sz, pa_x, rx_px, pa_z, rx_pz,
           unit_own, unit_par, unit_t, acc, normed_b, slope_b, part,
           sbuf, ra, rb, fsend, frecv, lsend, lrecv,
           wsem, zsem, zrsem, esem, ersem, gsem, grsem, usem, ursem,
           sxs, sxr, szs, szr, pxs, pxr, pzs, pzr,
           ssem, rasem, rbsem, fsem, frsem, ysem, yrsem):
    s = lax.axis_index("section")
    z = lax.axis_index("gy")
    me = lax.axis_index("gx")
    core = me % 2
    xc = me // 2
    partner = xc * 2 + 1 - core

    wcopy = pltpu.make_async_copy(w_hbm, wbuf, wsem)
    wcopy.start()

    barrier = pltpu.get_barrier_semaphore()
    for d in range(1, 8):
        pl.semaphore_signal(barrier, inc=1, device_id={"gx": (me + d) % 8}, device_id_type=MESH)
        pl.semaphore_signal(barrier, inc=1, device_id={"gy": (z + d) % 8}, device_id_type=MESH)

    @pl.when(s > 0)
    def _():
        pl.semaphore_signal(barrier, inc=1, device_id={"section": s - 1}, device_id_type=MESH)

    @pl.when(s < 3)
    def _():
        pl.semaphore_signal(barrier, inc=1, device_id={"section": s + 1}, device_id_type=MESH)

    def stat_body(i, carry):
        a, b = carry
        v = x_ref[pl.ds(pl.multiple_of(i * 64, 64), 64), :].astype(F32)
        return a + jnp.sum(v.reshape(8, 8, 320), axis=0), b + jnp.sum((v * v).reshape(8, 8, 320), axis=0)

    zero8 = jnp.zeros((8, 320), F32)
    a, b = lax.fori_loop(0, 8, stat_body, (zero8, zero8))
    st_x[...] = zero8
    st_x[0:1, :] = jnp.sum(a, axis=0, keepdims=True)
    st_x[1:2, :] = jnp.sum(b, axis=0, keepdims=True)

    first_entry = 14 + jnp.where(s > 0, 1, 0) + jnp.where(s < 3, 1, 0)
    pl.semaphore_wait(barrier, first_entry)

    def gather(src, dst, ssems, rsems, axis, at):
        out = []
        for d in range(1, 8):
            to = (at + d) % 8
            out.append(pltpu.make_async_remote_copy(
                src_ref=src, dst_ref=dst.at[at], send_sem=ssems.at[d], recv_sem=rsems.at[at],
                device_id={axis: to}, device_id_type=MESH))
            out[-1].start()
        dst[pl.ds(at, 1)] = src[...][None]

    def gathered(src, dst, ssems, rsems, axis, at):
        for d in range(1, 8):
            frm = (at + d) % 8
            cp = pltpu.make_async_remote_copy(
                src_ref=src, dst_ref=dst.at[frm], send_sem=ssems.at[d], recv_sem=rsems.at[frm],
                device_id={axis: frm}, device_id_type=MESH)
            cp.wait_send()
            cp.wait_recv()
        tot = dst[0]
        for d in range(1, 8):
            tot = tot + dst[d]
        return tot

    def halo(src_row, dst_row, to, i):
        return pltpu.make_async_remote_copy(
            src_ref=g_ref.at[:, pl.ds(src_row, 16), :],
            dst_ref=gs.at[1, pl.ds(1, 4), pl.ds(dst_row, 16), :],
            send_sem=zsem.at[i], recv_sem=zrsem.at[i], device_id={"gy": to}, device_id_type=MESH)

    up_halo = halo(0, 144, jnp.maximum(z - 1, 0), 0)
    down_halo = halo(112, 0, jnp.minimum(z + 1, 7), 1)
    pl.when(z > 0)(lambda: up_halo.start())
    pl.when(z < 7)(lambda: down_halo.start())
    gather(st_x, rx_sx, sxs, sxr, "gx", me)

    zrow = jnp.zeros((4, 16, 320), BF16)
    for c in range(3):
        gs[c, 0] = jnp.zeros((160, 320), BF16)
        gs[c, 5] = jnp.zeros((160, 320), BF16)

    @pl.when(z == 0)
    def _():
        gs[1, 1:5, 0:16, :] = zrow

    @pl.when(z == 7)
    def _():
        gs[1, 1:5, 144:160, :] = zrow

    bsum = jnp.zeros((1, 320), F32)
    for f in range(4):
        v = g_ref[f]
        gs[1, 1 + f, 16:144, :] = v
        v = v.astype(F32)
        bsum = bsum + jnp.sum(v, axis=0, keepdims=True)
    pa_x[...] = zero8
    pa_x[2:3, :] = bsum

    @pl.when(z > 0)
    def _():
        up_halo.wait_send()
        down_halo.wait_recv()

    @pl.when(z < 7)
    def _():
        down_halo.wait_send()
        up_halo.wait_recv()

    for f in range(4):
        v = gs[1, 1 + f].astype(F32)
        gf[f, 0] = v[:, 0:128]
        gf[f, 1] = v[:, 128:256]
        gf[f, 2] = jnp.concatenate([v[:, 256:320], jnp.zeros((160, 64), F32)], axis=1)
    for f in range(4):
        for l in range(3):
            edge_out[0, f, l] = jnp.zeros((16, 128), F32)
            edge_out[1, f, l] = jnp.zeros((16, 128), F32)
            edge_out[0, f, l, 0:10, :] = gf[f, l, pl.ds(0, 10, stride=16), :]
            edge_out[1, f, l, 0:10, :] = gf[f, l, pl.ds(15, 10, stride=16), :]
    to_left = pltpu.make_async_remote_copy(
        src_ref=edge_out.at[0], dst_ref=edge_r, send_sem=esem.at[0], recv_sem=ersem.at[0],
        device_id={"gx": jnp.maximum(me - 1, 0)}, device_id_type=MESH)
    to_right = pltpu.make_async_remote_copy(
        src_ref=edge_out.at[1], dst_ref=edge_l, send_sem=esem.at[1], recv_sem=ersem.at[1],
        device_id={"gx": jnp.minimum(me + 1, 7)}, device_id_type=MESH)
    pl.when(me > 0)(lambda: to_left.start())
    pl.when(me < 7)(lambda: to_right.start())

    @pl.when(me == 0)
    def _():
        edge_l[...] = jnp.zeros((4, 3, 16, 128), F32)

    @pl.when(me == 7)
    def _():
        edge_r[...] = jnp.zeros((4, 3, 16, 128), F32)

    st_z[...] = gathered(st_x, rx_sx, sxs, sxr, "gx", me)
    gather(st_z, rx_sz, szs, szr, "gy", z)

    @pl.when(me > 0)
    def _():
        to_left.wait_send()
        to_right.wait_recv()

    @pl.when(me < 7)
    def _():
        to_right.wait_send()
        to_left.wait_recv()

    for f in range(4):
        for l in range(3):
            w = 128 if l < 2 else 64
            v = gf[f, l]
            tmp[0] = pltpu.roll(v, 1, 0)
            tmp[1] = pltpu.roll(v, 159, 0)
            tmp[0, pl.ds(0, 10, stride=16), :] = edge_l[f, l, 0:10, :]
            tmp[1, pl.ds(15, 10, stride=16), :] = edge_r[f, l, 0:10, :]
            gs[2, 1 + f, :, 128 * l:128 * l + w] = tmp[0, :, 0:w].astype(BF16)
            gs[0, 1 + f, :, 128 * l:128 * l + w] = tmp[1, :, 0:w].astype(BF16)
    swap = pltpu.make_async_remote_copy(
        src_ref=gs, dst_ref=pgs, send_sem=gsem, recv_sem=grsem,
        device_id={"gx": partner}, device_id_type=MESH)
    swap.start()

    wcopy.wait()

    def window(ref, c, a, b):
        v = ref[c, pl.ds(2 - a, 4), pl.ds(pl.multiple_of((2 - b) * 16, 16), 128), :]
        return v.reshape(512, 320)

    def side(ab, first):
        a, b = ab // 3, ab % 3
        tot = None
        for c in range(3):
            wk = wbuf[ab * 3 + c]
            d = lax.dot_general(window(gs, c, a, b), wk, (((1,), (1,)), ((), ())), preferred_element_type=F32)
            tot = d if tot is None else tot + d
        acc[...] += tot
        return first

    acc[...] = jnp.zeros((512, 320), F32)
    lax.fori_loop(0, 9, side, 0)

    tot = gathered(st_z, rx_sz, szs, szr, "gy", z)
    members = float(512 * 64 * 10)
    grp = grp_ref[...]
    per = jnp.dot(tot, grp, precision=lax.Precision.HIGHEST, preferred_element_type=F32) / members
    mean = per[0:1, :]
    var = per[1:2, :] - mean * mean
    inv = 1.0 / jnp.sqrt(var + EPS)
    gain = gain_ref[...]
    shift = shift_ref[...]

    def act_body(i, carry):
        p0, p1 = carry
        rows = pl.ds(pl.multiple_of(i * 32, 32), 32)
        n = (x_ref[rows, :].astype(F32) - mean) * inv
        y = n * gain + shift
        sg = jax.nn.sigmoid(y)
        unit_own[rows, :] = (y * sg).astype(BF16)
        ag = acc[rows, :] * (sg * (1.0 + y * (1.0 - sg)))
        acc[rows, :] = ag
        normed_b[rows, :] = n
        return p0 + jnp.sum((ag * n).reshape(4, 8, 320), axis=0), p1 + jnp.sum(ag.reshape(4, 8, 320), axis=0)

    p0, p1 = lax.fori_loop(0, 16, act_body, (zero8, zero8))
    swap_u = pltpu.make_async_remote_copy(
        src_ref=unit_own, dst_ref=unit_par, send_sem=usem, recv_sem=ursem,
        device_id={"gx": partner}, device_id_type=MESH)
    swap_u.start()
    pa_x[0:1, :] = jnp.sum(p0, axis=0, keepdims=True)
    pa_x[1:2, :] = jnp.sum(p1, axis=0, keepdims=True)
    gather(pa_x, rx_px, pxs, pxr, "gx", me)

    unit_t[:, 0:512] = unit_own[...].T
    swap.wait()
    swap_u.wait()
    unit_t[:, 512:1024] = unit_par[...].T
    pa_z[...] = gathered(pa_x, rx_px, pxs, pxr, "gx", me)
    gather(pa_z, rx_pz, pzs, pzr, "gy", z)

    def taps(t, carry):
        k = 13 * core + t
        ab = k // 3
        c = k % 3
        a, b = ab // 3, ab % 3
        win = jnp.concatenate([window(gs, c, a, b), window(pgs, c, a, b)], axis=0)
        part[pl.ds(pl.multiple_of(t * 320, 64), 320), :] = jnp.dot(unit_t[...], win, preferred_element_type=F32)
        return carry

    lax.fori_loop(0, 14, taps, 0)

    def base_of(j):
        return pl.multiple_of(160 * core + SLAB * j, 8)

    def hop(j, i, up):
        to = jnp.where(up, z + 1, z + 7) % 8
        return to

    def step(tau, carry):
        def one(j, c2):
            delta = (4 * core + j - z + 8) % 8
            for i in range(SUB):
                top = 4 - (i % 2)
                going_up = (delta >= 1) & (delta <= top)
                going_down = delta > top
                when_up = top - delta
                when_down = delta - top - 1
                rows = pl.ds(pl.multiple_of(base_of(j) + ROWS * i, 8), ROWS)

                def sends_up(j=j, i=i):
                    return pltpu.make_async_remote_copy(
                        src_ref=sbuf.at[j, i], dst_ref=ra.at[j, i], send_sem=ssem.at[j, i],
                        recv_sem=rasem.at[j, i], device_id={"gy": (z + 1) % 8}, device_id_type=MESH)

                def sends_down(j=j, i=i):
                    return pltpu.make_async_remote_copy(
                        src_ref=sbuf.at[j, i], dst_ref=rb.at[j, i], send_sem=ssem.at[j, i],
                        recv_sem=rbsem.at[j, i], device_id={"gy": (z + 7) % 8}, device_id_type=MESH)

                @pl.when(going_up & (when_up == tau))
                def _():
                    @pl.when(tau == 0)
                    def _():
                        sbuf[j, i] = part[rows, :].astype(BF16)

                    @pl.when(tau > 0)
                    def _():
                        sends_up().wait_recv()
                        sbuf[j, i] = (part[rows, :] + ra[j, i].astype(F32)).astype(BF16)

                    sends_up().start()

                @pl.when(going_down & (when_down == tau))
                def _():
                    @pl.when(tau == 0)
                    def _():
                        sbuf[j, i] = part[rows, :].astype(BF16)

                    @pl.when(tau > 0)
                    def _():
                        sends_down().wait_recv()
                        sbuf[j, i] = (part[rows, :] + rb[j, i].astype(F32)).astype(BF16)

                    sends_down().start()

                @pl.when((delta == 0) & (tau == 4))
                def _():
                    sends_up().wait_recv()
                    sends_down().wait_recv()
                    part[rows, :] = part[rows, :] + ra[j, i].astype(F32) + rb[j, i].astype(F32)

            return c2

        lax.fori_loop(0, 4, one, 0)
        return carry

    step(0, 0)

    ptot = gathered(pa_z, rx_pz, pzs, pzr, "gy", z)
    par_ref[...] = ptot[0:3, :]
    gg = jnp.dot(ptot * gain, grp, precision=lax.Precision.HIGHEST, preferred_element_type=F32) / members
    second = gg[0:1, :]
    first = gg[1:2, :]

    def lev(i, carry):
        rows = pl.ds(pl.multiple_of(i * 32, 32), 32)
        gv = g_ref[i // 4, pl.ds(pl.multiple_of((i % 4) * 32, 32), 32), :].astype(F32)
        ng = (acc[rows, :] * gain - first - normed_b[rows, :] * second) * inv
        lsend[rows, :] = (gv + ng).astype(BF16)
        return carry

    lax.fori_loop(0, 16, lev, 0)
    ycopy = pltpu.make_async_remote_copy(
        src_ref=lsend, dst_ref=lrecv, send_sem=ysem, recv_sem=yrsem,
        device_id={"section": jnp.maximum(s - 1, 0)}, device_id_type=MESH)
    pl.when(s > 0)(lambda: ycopy.start())

    lax.fori_loop(1, 5, step, 0)

    root = z // 4

    @pl.when(core == root)
    def _():
        j = z - 4 * core
        for d in range(8):
            lo = (135 * d) // 8 * 8
            v = part[pl.ds(pl.multiple_of(base_of(j) + lo, 8), 144 if d < 7 else 136), :]
            fsend[d, 0:135, :] = v[135 * d - lo:135 * d - lo + 135, :]
        for d in range(1, 8):
            to = (me + d) % 8
            pltpu.make_async_remote_copy(
                src_ref=fsend.at[to], dst_ref=frecv.at[xc], send_sem=fsem.at[d], recv_sem=frsem.at[xc],
                device_id={"gx": to}, device_id_type=MESH).start()
        frecv[pl.ds(xc, 1)] = fsend[pl.ds(me, 1)]

    for q in range(4):
        src = 2 * q + root

        @pl.when(src != me)
        def _(q=q):
            pltpu.make_async_remote_copy(
                src_ref=fsend.at[q], dst_ref=frecv.at[q], send_sem=fsem.at[0], recv_sem=frsem.at[q],
                device_id={"gx": partner}, device_id_type=MESH).wait_recv()

    tot = frecv[0, 0:135, :]
    for q in range(1, 4):
        tot = tot + frecv[q, 0:135, :]
    dw_ref[...] = tot

    @pl.when(core == root)
    def _():
        for d in range(1, 8):
            pltpu.make_async_remote_copy(
                src_ref=fsend.at[d], dst_ref=frecv.at[0], send_sem=fsem.at[d], recv_sem=frsem.at[0],
                device_id={"gx": (me + d) % 8}, device_id_type=MESH).wait_send()

    def drain(j, carry):
        delta = (4 * core + j - z + 8) % 8

        @pl.when(delta != 0)
        def _():
            for i in range(SUB):
                pltpu.make_async_remote_copy(
                    src_ref=sbuf.at[j, i], dst_ref=ra.at[j, i], send_sem=ssem.at[j, i],
                    recv_sem=rasem.at[j, i], device_id={"gy": (z + 1) % 8}, device_id_type=MESH).wait_send()

        return carry

    lax.fori_loop(0, 4, drain, 0)
    pl.when(s > 0)(lambda: ycopy.wait_send())

    @pl.when(s < 3)
    def _():
        ycopy.wait_recv()
        up_ref[...] = lrecv[...]

    @pl.when(s == 3)
    def _():
        up_ref[...] = jnp.zeros((512, 320), BF16)


def local(level_input, out_grad, conv_weight, norm_gain, norm_shift):
    grp = jnp.kron(jnp.eye(G, dtype=F32), jnp.ones((10, 10), F32))
    vm = pl.BlockSpec(memory_space=pltpu.VMEM)
    dma = pltpu.SemaphoreType.DMA
    V = pltpu.VMEM
    up, dw, par = pl.pallas_call(
        kernel,
        out_shape=(
            jax.ShapeDtypeStruct((512, 320), BF16),
            jax.ShapeDtypeStruct((135, 320), F32),
            jax.ShapeDtypeStruct((3, 320), F32),
        ),
        in_specs=[vm, vm, pl.BlockSpec(memory_space=pl.ANY), vm, vm, vm],
        out_specs=(vm, vm, vm),
        scratch_shapes=[
            V((27, 320, 320), BF16), V((3, 6, 160, 320), BF16), V((3, 6, 160, 320), BF16),
            V((4, 3, 160, 128), F32), V((2, 160, 128), F32),
            V((2, 4, 3, 16, 128), F32), V((4, 3, 16, 128), F32), V((4, 3, 16, 128), F32),
            V((8, 320), F32), V((8, 8, 320), F32), V((8, 320), F32), V((8, 8, 320), F32),
            V((8, 320), F32), V((8, 8, 320), F32), V((8, 320), F32), V((8, 8, 320), F32),
            V((512, 320), BF16), V((512, 320), BF16), V((320, 1024), BF16),
            V((512, 320), F32), V((512, 320), F32), V((8, 320), F32), V((14 * 320, 320), F32),
            V((4, SUB, ROWS, 320), BF16), V((4, SUB, ROWS, 320), BF16), V((4, SUB, ROWS, 320), BF16),
            V((8, 136, 320), F32), V((4, 136, 320), F32),
            V((512, 320), BF16), V((512, 320), BF16),
            dma(()), dma((2,)), dma((2,)), dma((2,)), dma((2,)), dma(()), dma(()), dma(()), dma(()),
            dma((8,)), dma((8,)), dma((8,)), dma((8,)), dma((8,)), dma((8,)), dma((8,)), dma((8,)),
            dma((4, SUB)), dma((4, SUB)), dma((4, SUB)), dma((8,)), dma((4,)), dma(()), dma(()),
        ],
        compiler_params=pltpu.CompilerParams(
            collective_id=0, has_side_effects=True, vmem_limit_bytes=60 * 1024 * 1024
        ),
    )(
        level_input.reshape(512, 320), out_grad.reshape(4, 128, 320), conv_weight.reshape(27, 320, 320),
        norm_gain, norm_shift, grp,
    )
    return up.reshape(1, 4, 8, 16, 320), dw[None], par[None]


def solution(mesh):
    return jax.shard_map(
        local,
        mesh=mesh,
        in_specs=(
            P("section", None, "gy", "gx", None),
            P("section", None, "gy", "gx", None),
            P("section", None, None, None),
            P("section", None),
            P("section", None),
        ),
        out_specs=(
            P("section", None, "gy", "gx", None),
            P("section", ("gy", "gx"), None),
            P("section", None, None),
        ),
        check_vma=False,
    )
```

time: 337 us -> 102 us (0.30)
  the two profiles are of different devices: /device:TPU:8 before, /device:TPU:113 now
where the time goes in v1:
time: 102 us
  Pallas kernels  87.6 us (86%)
  local copies, waits for them, and re-layouts  14 us (14%)
    pallas_call x1, Pallas kernels, local(): pl.pallas_call(kernel, out_shape=(jax.ShapeDtypeStruct((512, 320), BF16),...  87.6 us
    mul x2, local copies, waits for them, and re-layouts, local(): grp = jnp.kron(jnp.eye(G, dtype=F32), jnp.ones((10, 10), F32))  9.1 us
    unnamed x3, local copies, waits for them, and re-layouts  4.89 us

profile of v1, /device:TPU:113, one launch (start us, length us, event | category | flops | bytes accessed | tf_op | source)
XLA Modules:
  0.0 102.3 jit_solution(17444081296076500814)
XLA Ops:
  0.6 3.0 %mul.19 = f32[32,10,32,10]{3,2,1,0:T(8,128)} broadcast(f32[32,32]{1,0:T(8,128)S(1)} %fusion), dimensions={0,2} | broadcast | bytes 413696 | tf_op jit(solution)/shard_map/jit(kron)/mul | solution.py:408
  3.7 6.1 %mul.20.grp_ref = f32[320,320]{1,0:T(8,128)} reshape(f32[32,10,32,10]{3,2,1,0:T(8,128)} %mul.19) | data formatting | bytes 819200 | tf_op jit(solution)/shard_map/jit(kron)/mul | solution.py:408
  9.7 87.6 %shard_map.76 = (bf16[512,320]{1,0:T(8,128)(2,1)}, f32[135,320]{1,0:T(8,128)}, f32[3,320]{1,0:T(4,128)}) custom-call(bf16[512,320]{1,0:T(8,128)(2,1)} %bitcast.9, bf16[4,128,320]{2,1,0:T(8,128)(2,1)} %bitcast.10, bf16[27,320,320]{2,1,0:T(8,128)(2,1)} %bitcast.8, f32[1,320]{1,0:T(1,128)} %gain_ref.1, f32[1,320]{1,0:T(1,128)} %shift_ref.1, f32[320,320]{1,0:T(8,128)} %mul.20.grp_ref), custom_call_target="tpu_custom_call" | custom-call | tf_op jit(solution)/shard_map/pallas_call | solution.py:412
  97.4 1.8 %copy.10 = f32[1,135,320]{2,0,1:T(1,128)} copy(f32[1,135,320]{2,1,0:T(8,128)} %bitcast.12) | data formatting | bytes 345600
  99.2 1.3 %copy.11 = f32[1,3,320]{2,0,1:T(1,128)} copy(f32[1,3,320]{2,1,0:T(4,128)} %bitcast.13) | data formatting | bytes 7680
  100.5 1.8 %copy.13 = bf16[1,4,8,16,320]{4,3,2,1,0:T(8,128)(2,1)} copy(bf16[1,4,8,16,320]{4,3,2,1,0:T(8,128)(2,1)} %bitcast.11) | data formatting | bytes 655360
  (1 shorter events, 0.0 us)

commit v2 on v1

v2 whole, which is shorter than its diff:
```python
import jax
import jax.numpy as jnp
from jax import lax
from jax.experimental import pallas as pl
from jax.experimental.pallas import tpu as pltpu
from jax.sharding import PartitionSpec as P

G = 32
EPS = 1e-05
MESH = pl.DeviceIdType.MESH
SLAB = 1080
F32 = jnp.float32
BF16 = jnp.bfloat16


def pack(u):
    rem = u[:, 256:320]
    wide = jnp.concatenate([rem[0:72], jnp.concatenate([rem[72:136], jnp.zeros((8, 64), F32)], axis=0)], axis=1)
    low = jnp.concatenate([wide[40:72], jnp.zeros((8, 128), F32)], axis=0)
    return u[:, 0:256], jnp.concatenate([wide[0:40], low], axis=1)


def unpack(t):
    q = t[136:176]
    wide = jnp.concatenate([q[:, 0:128], q[0:32, 128:256]], axis=0)
    rem = jnp.concatenate([wide[:, 0:64], wide[0:64, 64:128]], axis=0)
    return jnp.concatenate([t[0:136], rem], axis=1)[0:135]


def kernel(x_ref, g_ref, w_hbm, gain_ref, shift_ref,
           up_ref, dw_ref, par_ref,
           wbuf, gs, pgs, gf, tmp, edge_out, edge_l, edge_r,
           st_x, rx_sx, st_z, rx_sz, pa_x, rx_px, pa_z, rx_pz,
           unit_own, unit_par, unit_t, acc, normed_b, slope_b, part, own,
           sbuf, ra, rb, bown, bs, bra, brb, xs, xm, xr, fsend, frecv, bfin, brecv, lsend, lrecv,
           wsem, zsem, zrsem, esem, ersem, gsem, grsem, usem, ursem,
           sxs, sxr, szs, szr, pxs, pxr, pzs, pzr,
           ssem, rasem, rbsem, bssem, brasem, brbsem, xssem, xmsem, xrsem,
           fsem, frsem, bfsem, bfrsem, ysem, yrsem):
    s = lax.axis_index("section")
    z = lax.axis_index("gy")
    me = lax.axis_index("gx")
    core = me % 2
    xc = me // 2
    partner = xc * 2 + 1 - core

    wcopy = pltpu.make_async_copy(w_hbm, wbuf, wsem)
    wcopy.start()

    barrier = pltpu.get_barrier_semaphore()
    for d in range(1, 8):
        pl.semaphore_signal(barrier, inc=1, device_id={"gx": (me + d) % 8}, device_id_type=MESH)
        pl.semaphore_signal(barrier, inc=1, device_id={"gy": (z + d) % 8}, device_id_type=MESH)

    @pl.when(s > 0)
    def _():
        pl.semaphore_signal(barrier, inc=1, device_id={"section": s - 1}, device_id_type=MESH)

    @pl.when(s < 3)
    def _():
        pl.semaphore_signal(barrier, inc=1, device_id={"section": s + 1}, device_id_type=MESH)

    def stat_body(i, carry):
        a, b = carry
        v = x_ref[pl.ds(pl.multiple_of(i * 64, 64), 64), :].astype(F32)
        return a + jnp.sum(v.reshape(8, 8, 320), axis=0), b + jnp.sum((v * v).reshape(8, 8, 320), axis=0)

    zero8 = jnp.zeros((8, 320), F32)
    a, b = lax.fori_loop(0, 8, stat_body, (zero8, zero8))
    st_x[...] = zero8
    st_x[0:1, :] = jnp.sum(a, axis=0, keepdims=True)
    st_x[1:2, :] = jnp.sum(b, axis=0, keepdims=True)

    first_entry = 14 + jnp.where(s > 0, 1, 0) + jnp.where(s < 3, 1, 0)
    pl.semaphore_wait(barrier, first_entry)

    def gather(src, dst, ssems, rsems, axis, at):
        out = []
        for d in range(1, 8):
            to = (at + d) % 8
            out.append(pltpu.make_async_remote_copy(
                src_ref=src, dst_ref=dst.at[at], send_sem=ssems.at[d], recv_sem=rsems.at[at],
                device_id={axis: to}, device_id_type=MESH))
            out[-1].start()
        dst[pl.ds(at, 1)] = src[...][None]

    def gathered(src, dst, ssems, rsems, axis, at):
        for d in range(1, 8):
            frm = (at + d) % 8
            cp = pltpu.make_async_remote_copy(
                src_ref=src, dst_ref=dst.at[frm], send_sem=ssems.at[d], recv_sem=rsems.at[frm],
                device_id={axis: frm}, device_id_type=MESH)
            cp.wait_send()
            cp.wait_recv()
        tot = dst[0]
        for d in range(1, 8):
            tot = tot + dst[d]
        return tot

    def halo(src_row, dst_row, to, i):
        return pltpu.make_async_remote_copy(
            src_ref=g_ref.at[:, pl.ds(src_row, 16), :],
            dst_ref=gs.at[1, pl.ds(1, 4), pl.ds(dst_row, 16), :],
            send_sem=zsem.at[i], recv_sem=zrsem.at[i], device_id={"gy": to}, device_id_type=MESH)

    up_halo = halo(0, 144, jnp.maximum(z - 1, 0), 0)
    down_halo = halo(112, 0, jnp.minimum(z + 1, 7), 1)
    pl.when(z > 0)(lambda: up_halo.start())
    pl.when(z < 7)(lambda: down_halo.start())
    gather(st_x, rx_sx, sxs, sxr, "gx", me)

    zrow = jnp.zeros((4, 16, 320), BF16)
    part[14 * 320:14 * 320 + 8, :] = zero8
    for c in range(3):
        pgs[c, 0] = jnp.zeros((160, 320), BF16)
        pgs[c, 5] = jnp.zeros((160, 320), BF16)
        gs[c, 0] = jnp.zeros((160, 320), BF16)
        gs[c, 5] = jnp.zeros((160, 320), BF16)

    @pl.when(z == 0)
    def _():
        gs[1, 1:5, 0:16, :] = zrow

    @pl.when(z == 7)
    def _():
        gs[1, 1:5, 144:160, :] = zrow

    bsum = jnp.zeros((1, 320), F32)
    for f in range(4):
        v = g_ref[f]
        gs[1, 1 + f, 16:144, :] = v
        v = v.astype(F32)
        bsum = bsum + jnp.sum(v, axis=0, keepdims=True)
    pa_x[...] = zero8
    pa_x[2:3, :] = bsum

    @pl.when(z > 0)
    def _():
        up_halo.wait_send()
        down_halo.wait_recv()

    @pl.when(z < 7)
    def _():
        down_halo.wait_send()
        up_halo.wait_recv()

    for f in range(4):
        v = gs[1, 1 + f].astype(F32)
        gf[f, 0] = v[:, 0:128]
        gf[f, 1] = v[:, 128:256]
        gf[f, 2] = jnp.concatenate([v[:, 256:320], jnp.zeros((160, 64), F32)], axis=1)
    for f in range(4):
        for l in range(3):
            edge_out[0, f, l] = jnp.zeros((16, 128), F32)
            edge_out[1, f, l] = jnp.zeros((16, 128), F32)
            edge_out[0, f, l, 0:10, :] = gf[f, l, pl.ds(0, 10, stride=16), :]
            edge_out[1, f, l, 0:10, :] = gf[f, l, pl.ds(15, 10, stride=16), :]
    to_left = pltpu.make_async_remote_copy(
        src_ref=edge_out.at[0], dst_ref=edge_r, send_sem=esem.at[0], recv_sem=ersem.at[0],
        device_id={"gx": jnp.maximum(me - 1, 0)}, device_id_type=MESH)
    to_right = pltpu.make_async_remote_copy(
        src_ref=edge_out.at[1], dst_ref=edge_l, send_sem=esem.at[1], recv_sem=ersem.at[1],
        device_id={"gx": jnp.minimum(me + 1, 7)}, device_id_type=MESH)
    pl.when(me > 0)(lambda: to_left.start())
    pl.when(me < 7)(lambda: to_right.start())

    @pl.when(me == 0)
    def _():
        edge_l[...] = jnp.zeros((4, 3, 16, 128), F32)

    @pl.when(me == 7)
    def _():
        edge_r[...] = jnp.zeros((4, 3, 16, 128), F32)

    st_z[...] = gathered(st_x, rx_sx, sxs, sxr, "gx", me)
    gather(st_z, rx_sz, szs, szr, "gy", z)

    @pl.when(me > 0)
    def _():
        to_left.wait_send()
        to_right.wait_recv()

    @pl.when(me < 7)
    def _():
        to_right.wait_send()
        to_left.wait_recv()

    for f in range(4):
        for l in range(3):
            w = 128 if l < 2 else 64
            v = gf[f, l]
            tmp[0] = pltpu.roll(v, 1, 0)
            tmp[1] = pltpu.roll(v, 159, 0)
            tmp[0, pl.ds(0, 10, stride=16), :] = edge_l[f, l, 0:10, :]
            tmp[1, pl.ds(15, 10, stride=16), :] = edge_r[f, l, 0:10, :]
            gs[2, 1 + f, :, 128 * l:128 * l + w] = tmp[0, :, 0:w].astype(BF16)
            gs[0, 1 + f, :, 128 * l:128 * l + w] = tmp[1, :, 0:w].astype(BF16)
    swap = pltpu.make_async_remote_copy(
        src_ref=gs.at[:, pl.ds(1, 4)], dst_ref=pgs.at[:, pl.ds(1, 4)], send_sem=gsem, recv_sem=grsem,
        device_id={"gx": partner}, device_id_type=MESH)
    swap.start()

    def window(ref, c, a, b):
        v = ref[c, pl.ds(2 - a, 4), pl.ds(pl.multiple_of((2 - b) * 16, 16), 128), :]
        return v.reshape(512, 320)

    ia = jnp.floor((lax.broadcasted_iota(jnp.int32, (320, 320), 0).astype(F32) + 0.5) * 0.1)
    ib = jnp.floor((lax.broadcasted_iota(jnp.int32, (320, 320), 1).astype(F32) + 0.5) * 0.1)
    grp = jnp.where(ia == ib, 1.0, 0.0).astype(F32)
    members = float(512 * 64 * 10)
    tot = gathered(st_z, rx_sz, szs, szr, "gy", z)
    per = jnp.dot(tot, grp, precision=lax.Precision.HIGHEST, preferred_element_type=F32) / members
    mean = per[0:1, :]
    var = per[1:2, :] - mean * mean
    inv = 1.0 / jnp.sqrt(var + EPS)
    gain = gain_ref[...]
    shift = shift_ref[...]

    def act_body(i, carry):
        rows = pl.ds(pl.multiple_of(i * 64, 64), 64)
        n = (x_ref[rows, :].astype(F32) - mean) * inv
        y = n * gain + shift
        sg = jax.nn.sigmoid(y)
        unit_own[rows, :] = (y * sg).astype(BF16)
        slope_b[rows, :] = sg * (1.0 + y * (1.0 - sg))
        normed_b[rows, :] = n
        return carry

    lax.fori_loop(0, 8, act_body, 0)
    swap_u = pltpu.make_async_remote_copy(
        src_ref=unit_own, dst_ref=unit_par, send_sem=usem, recv_sem=ursem,
        device_id={"gx": partner}, device_id_type=MESH)
    swap_u.start()
    unit_t[:, 0:512] = unit_own[...].T
    swap.wait()
    swap_u.wait()
    unit_t[:, 512:1024] = unit_par[...].T

    def taps(t, carry):
        k = 13 * core + t
        ab = k // 3
        c = k % 3
        a, b = ab // 3, ab % 3
        win = jnp.concatenate([window(gs, c, a, b), window(pgs, c, a, b)], axis=0)
        part[pl.ds(pl.multiple_of(t * 320, 64), 320), :] = jnp.dot(unit_t[...], win, preferred_element_type=F32)
        return carry

    lax.fori_loop(0, 14, taps, 0)

    def packing(j, carry):
        for d in range(8):
            lo = (135 * d) // 8 * 8
            v = part[pl.ds(pl.multiple_of(160 * core + SLAB * j + lo, 8), 144), :]
            main, rest = pack(v[135 * d - lo:135 * d - lo + 136, :])
            own[j, d, 0:136, :] = main
            own[j, d, 136:176, :] = rest
        return carry

    lax.fori_loop(0, 4, packing, 0)

    def relay(j, tau, top, mine, sb, up_in, down_in, s_send, s_up, s_down, result):
        delta = (4 * core + j - z + 8) % 8
        going_up = (delta >= 1) & (delta <= top)
        going_down = delta > top

        def sends_up():
            return pltpu.make_async_remote_copy(
                src_ref=sb, dst_ref=up_in, send_sem=s_send, recv_sem=s_up,
                device_id={"gy": (z + 1) % 8}, device_id_type=MESH)

        def sends_down():
            return pltpu.make_async_remote_copy(
                src_ref=sb, dst_ref=down_in, send_sem=s_send, recv_sem=s_down,
                device_id={"gy": (z + 7) % 8}, device_id_type=MESH)

        for cond, when, send, got in (
            (going_up, top - delta, sends_up, up_in),
            (going_down, delta - top - 1, sends_down, down_in),
        ):
            @pl.when(cond & (when == tau))
            def _(send=send, got=got):
                if tau == 0:
                    sb[...] = mine[...].astype(sb.dtype)
                else:
                    send().wait_recv()
                    sb[...] = (mine[...] + got[...].astype(F32)).astype(sb.dtype)
                send().start()

        if tau == 4:
            @pl.when(delta == 0)
            def _():
                sends_up().wait_recv()
                sends_down().wait_recv()
                result[...] = mine[...] + up_in[...].astype(F32) + down_in[...].astype(F32)

    def chain_a(tau):
        def one(j, carry):
            for i in range(4):
                relay(j, tau, 4 - i % 2, own.at[j, 2 * i], sbuf.at[j, i], ra.at[j, i], rb.at[j, i],
                      ssem.at[j, i], rasem.at[j, i], rbsem.at[j, i], fsend.at[i])
            return carry

        lax.fori_loop(0, 4, one, 0)

    def chain_b(tau):
        for j in range(4):
            relay(j, tau, 4 - j % 2, bown.at[j], bs.at[j], bra.at[j], brb.at[j],
                  bssem.at[j], brasem.at[j], brbsem.at[j], bfin)

    def ring(j, e, dst, rsem):
        plus = e == 1 or (e == 2 and j % 2 == 0)
        to = ((xc + (1 if plus else 3)) % 4) * 2 + core
        return pltpu.make_async_remote_copy(
            src_ref=xs.at[j, e - 1], dst_ref=dst, send_sem=xssem.at[j, e - 1], recv_sem=rsem,
            device_id={"gx": to}, device_id_type=MESH)

    def odd(j, e):
        return own[j, 2 * ((xc + e) % 4) + 1]

    def long_in(j):
        return ring(j, 2, xm.at[j], xmsem.at[j])

    def root_in(j, e):
        return ring(j, e, xr.at[j, e // 2], xrsem.at[j, e // 2])

    def ring_0():
        for j in range(4):
            xs[j, 1] = odd(j, 2).astype(BF16)
            long_in(j).start()
        for j in range(4):
            e = 3 if j % 2 == 0 else 1
            xs[j, e - 1] = odd(j, e).astype(BF16)
            root_in(j, e).start()

    def ring_1():
        for j in range(4):
            e = 1 if j % 2 == 0 else 3
            long_in(j).wait_recv()
            xs[j, e - 1] = (odd(j, e) + xm[j].astype(F32)).astype(BF16)
            root_in(j, e).start()

    def ring_2():
        for j in range(4):
            root_in(j, 1).wait_recv()
            root_in(j, 3).wait_recv()
            bown[j] = odd(j, 0) + xr[j, 0].astype(F32) + xr[j, 1].astype(F32)

    chain_a(0)
    ring_0()

    wcopy.wait()

    def side(ab, carry):
        a, b = ab // 3, ab % 3
        tot = None
        for c in range(3):
            wk = wbuf[ab * 3 + c]
            d = lax.dot_general(window(gs, c, a, b), wk, (((1,), (1,)), ((), ())), preferred_element_type=F32)
            tot = d if tot is None else tot + d
        acc[...] += tot
        return carry

    acc[...] = jnp.zeros((512, 320), F32)
    lax.fori_loop(0, 9, side, 0)

    def grad_body(i, carry):
        p0, p1 = carry
        rows = pl.ds(pl.multiple_of(i * 64, 64), 64)
        ag = acc[rows, :] * slope_b[rows, :]
        acc[rows, :] = ag
        return (p0 + jnp.sum((ag * normed_b[rows, :]).reshape(8, 8, 320), axis=0),
                p1 + jnp.sum(ag.reshape(8, 8, 320), axis=0))

    p0, p1 = lax.fori_loop(0, 8, grad_body, (zero8, zero8))
    pa_x[0:1, :] = jnp.sum(p0, axis=0, keepdims=True)
    pa_x[1:2, :] = jnp.sum(p1, axis=0, keepdims=True)
    gather(pa_x, rx_px, pxs, pxr, "gx", me)

    ring_1()
    chain_a(1)
    pa_z[...] = gathered(pa_x, rx_px, pxs, pxr, "gx", me)
    gather(pa_z, rx_pz, pzs, pzr, "gy", z)
    ring_2()
    chain_b(0)
    chain_a(2)

    ptot = gathered(pa_z, rx_pz, pzs, pzr, "gy", z)
    par_ref[...] = ptot[0:3, :]
    gg = jnp.dot(ptot * gain, grp, precision=lax.Precision.HIGHEST, preferred_element_type=F32) / members
    second = gg[0:1, :]
    first = gg[1:2, :]

    def lev(i, carry):
        rows = pl.ds(pl.multiple_of(i * 64, 64), 64)
        gv = g_ref[i // 2, pl.ds(pl.multiple_of((i % 2) * 64, 64), 64), :].astype(F32)
        ng = (acc[rows, :] * gain - first - normed_b[rows, :] * second) * inv
        lsend[rows, :] = (gv + ng).astype(BF16)
        return carry

    lax.fori_loop(0, 8, lev, 0)
    ycopy = pltpu.make_async_remote_copy(
        src_ref=lsend, dst_ref=lrecv, send_sem=ysem, recv_sem=yrsem,
        device_id={"section": jnp.maximum(s - 1, 0)}, device_id_type=MESH)
    pl.when(s > 0)(lambda: ycopy.start())

    chain_b(1)
    chain_a(3)
    chain_b(2)
    chain_a(4)

    root = z // 4

    def to_even(x2):
        return pltpu.make_async_remote_copy(
            src_ref=fsend.at[x2], dst_ref=frecv.at[xc], send_sem=fsem.at[x2], recv_sem=frsem.at[xc],
            device_id={"gx": 2 * x2}, device_id_type=MESH)

    def to_odd():
        return pltpu.make_async_remote_copy(
            src_ref=bfin, dst_ref=brecv, send_sem=bfsem, recv_sem=bfrsem,
            device_id={"gx": partner}, device_id_type=MESH)

    for i in range(4):
        x2 = (xc + i) % 4
        if i:
            pl.when(core == root)(lambda x2=x2: to_even(x2).start())
        else:
            pl.when((core == root) & (core == 1))(lambda x2=x2: to_even(x2).start())

            @pl.when((core == root) & (core == 0))
            def _():
                frecv[pl.ds(xc, 1)] = fsend[pl.ds(xc, 1)]

    chain_b(3)
    chain_b(4)

    @pl.when((root == 0) & (core == 0))
    def _():
        to_odd().start()

    @pl.when((root == 1) & (core == 1))
    def _():
        dw_ref[...] = unpack(bfin[...])

    @pl.when((root == 0) & (core == 1))
    def _():
        to_odd().wait_recv()
        dw_ref[...] = unpack(brecv[...])

    @pl.when(core == 0)
    def _():
        for q in range(4):
            @pl.when((root == 1) | (xc != q))
            def _(q=q):
                pltpu.make_async_remote_copy(
                    src_ref=fsend.at[q], dst_ref=frecv.at[q], send_sem=fsem.at[q], recv_sem=frsem.at[q],
                    device_id={"gx": partner}, device_id_type=MESH).wait_recv()

        dw_ref[...] = unpack((frecv[0] + frecv[1]) + (frecv[2] + frecv[3]))

    for i in range(4):
        x2 = (xc + i) % 4
        if i:
            pl.when(core == root)(lambda x2=x2: to_even(x2).wait_send())
        else:
            pl.when((core == root) & (core == 1))(lambda x2=x2: to_even(x2).wait_send())

    @pl.when((root == 0) & (core == 0))
    def _():
        to_odd().wait_send()

    def drain(j, carry):
        @pl.when((4 * core + j - z + 8) % 8 != 0)
        def _():
            for i in range(4):
                pltpu.make_async_remote_copy(
                    src_ref=sbuf.at[j, i], dst_ref=ra.at[j, i], send_sem=ssem.at[j, i],
                    recv_sem=rasem.at[j, i], device_id={"gy": (z + 1) % 8}, device_id_type=MESH).wait_send()
            pltpu.make_async_remote_copy(
                src_ref=bs.at[j], dst_ref=bra.at[j], send_sem=bssem.at[j],
                recv_sem=brasem.at[j], device_id={"gy": (z + 1) % 8}, device_id_type=MESH).wait_send()

        return carry

    lax.fori_loop(0, 4, drain, 0)
    for j in range(4):
        long_in(j).wait_send()
        root_in(j, 1).wait_send()
        root_in(j, 3).wait_send()
    pl.when(s > 0)(lambda: ycopy.wait_send())

    @pl.when(s < 3)
    def _():
        ycopy.wait_recv()
        up_ref[...] = lrecv[...]

    @pl.when(s == 3)
    def _():
        up_ref[...] = jnp.zeros((512, 320), BF16)


def local(level_input, out_grad, conv_weight, norm_gain, norm_shift):
    vm = pl.BlockSpec(memory_space=pltpu.VMEM)
    dma = pltpu.SemaphoreType.DMA
    V = pltpu.VMEM
    up, dw, par = pl.pallas_call(
        kernel,
        out_shape=(
            jax.ShapeDtypeStruct((512, 320), BF16),
            jax.ShapeDtypeStruct((135, 320), F32),
            jax.ShapeDtypeStruct((3, 320), F32),
        ),
        in_specs=[vm, vm, pl.BlockSpec(memory_space=pl.ANY), vm, vm],
        out_specs=(vm, vm, vm),
        scratch_shapes=[
            V((27, 320, 320), BF16), V((3, 6, 160, 320), BF16), V((3, 6, 160, 320), BF16),
            V((4, 3, 160, 128), F32), V((2, 160, 128), F32),
            V((2, 4, 3, 16, 128), F32), V((4, 3, 16, 128), F32), V((4, 3, 16, 128), F32),
            V((8, 320), F32), V((8, 8, 320), F32), V((8, 320), F32), V((8, 8, 320), F32),
            V((8, 320), F32), V((8, 8, 320), F32), V((8, 320), F32), V((8, 8, 320), F32),
            V((512, 320), BF16), V((512, 320), BF16), V((320, 1024), BF16),
            V((512, 320), F32), V((512, 320), F32), V((512, 320), F32), V((14 * 320 + 8, 320), F32), V((4, 8, 176, 256), F32),
            V((4, 4, 176, 256), BF16), V((4, 4, 176, 256), BF16), V((4, 4, 176, 256), BF16),
            V((4, 176, 256), F32), V((4, 176, 256), F32), V((4, 176, 256), F32), V((4, 176, 256), F32),
            V((4, 3, 176, 256), BF16), V((4, 176, 256), BF16), V((4, 2, 176, 256), BF16),
            V((4, 176, 256), F32), V((4, 176, 256), F32), V((176, 256), F32), V((176, 256), F32),
            V((512, 320), BF16), V((512, 320), BF16),
            dma(()), dma((2,)), dma((2,)), dma((2,)), dma((2,)), dma(()), dma(()), dma(()), dma(()),
            dma((8,)), dma((8,)), dma((8,)), dma((8,)), dma((8,)), dma((8,)), dma((8,)), dma((8,)),
            dma((4, 4)), dma((4, 4)), dma((4, 4)), dma((4,)), dma((4,)), dma((4,)), dma((4, 3)), dma((4,)), dma((4, 2)),
            dma((4,)), dma((4,)), dma(()), dma(()), dma(()), dma(()),
        ],
        compiler_params=pltpu.CompilerParams(
            collective_id=0, has_side_effects=True, vmem_limit_bytes=60 * 1024 * 1024
        ),
    )(
        level_input.reshape(512, 320), out_grad.reshape(4, 128, 320), conv_weight.reshape(27, 320, 320),
        norm_gain, norm_shift,
    )
    return up.reshape(1, 4, 8, 16, 320), dw[None], par[None]


def solution(mesh):
    return jax.shard_map(
        local,
        mesh=mesh,
        in_specs=(
            P("section", None, "gy", "gx", None),
            P("section", None, "gy", "gx", None),
            P("section", None, None, None),
            P("section", None),
            P("section", None),
        ),
        out_specs=(
            P("section", None, "gy", "gx", None),
            P("section", ("gy", "gx"), None),
            P("section", None, None),
        ),
        check_vma=False,
    )
```

time: 102 us -> 77.3 us (0.76)
  the two profiles are of different devices: /device:TPU:113 before, /device:TPU:8 now
where the time goes in v2:
time: 77.3 us; the launch traced here: 76 us
  Pallas kernels  70.5 us (91%)
  local copies, waits for them, and re-layouts  4.89 us (6%)
    pallas_call x1, Pallas kernels, local(): pl.pallas_call(kernel, out_shape=(jax.ShapeDtypeStruct((512, 320), BF16),...  70.5 us
    unnamed x3, local copies, waits for them, and re-layouts  4.89 us

profile of v2, /device:TPU:8, one launch (start us, length us, event | category | flops | bytes accessed | tf_op | source)
XLA Modules:
  0.0 76.0 jit_solution(14485841468820827170)
XLA Ops:
  0.6 70.5 %shard_map.76 = (bf16[512,320]{1,0:T(8,128)(2,1)}, f32[135,320]{1,0:T(8,128)}, f32[3,320]{1,0:T(4,128)}) custom-call(bf16[512,320]{1,0:T(8,128)(2,1)} %bitcast.7, bf16[4,128,320]{2,1,0:T(8,128)(2,1)} %bitcast.8, bf16[27,320,320]{2,1,0:T(8,128)(2,1)} %bitcast.6, f32[1,320]{1,0:T(1,128)} %gain_ref.1, f32[1,320]{1,0:T(1,128)} %shift_ref.1), custom_call_target="tpu_custom_call" | custom-call | tf_op jit(solution)/shard_map/pallas_call | solution.py:506
  71.1 1.8 %copy.8 = f32[1,135,320]{2,0,1:T(1,128)} copy(f32[1,135,320]{2,1,0:T(8,128)} %bitcast.10) | data formatting | bytes 345600
  72.9 1.3 %copy.9 = f32[1,3,320]{2,0,1:T(1,128)} copy(f32[1,3,320]{2,1,0:T(4,128)} %bitcast.11) | data formatting | bytes 7680
  74.2 1.8 %copy.11 = bf16[1,4,8,16,320]{4,3,2,1,0:T(8,128)(2,1)} copy(bf16[1,4,8,16,320]{4,3,2,1,0:T(8,128)(2,1)} %bitcast.9) | data formatting | bytes 655360

commit v3 on v2

--- a/solution.py
+++ b/solution.py
@@ -32,10 +32,10 @@
            wbuf, gs, pgs, gf, tmp, edge_out, edge_l, edge_r,
            st_x, rx_sx, st_z, rx_sz, pa_x, rx_px, pa_z, rx_pz,
            unit_own, unit_par, unit_t, acc, normed_b, slope_b, part, own,
-           sbuf, ra, rb, bown, bs, bra, brb, xs, xm, xr, fsend, frecv, bfin, brecv, lsend, lrecv,
+           sbuf, ra, rb, bown, bs, bra, xs, xm, xr, fsend, frecv, bfin, brecv, lsend, lrecv,
            wsem, zsem, zrsem, esem, ersem, gsem, grsem, usem, ursem,
            sxs, sxr, szs, szr, pxs, pxr, pzs, pzr,
-           ssem, rasem, rbsem, bssem, brasem, brbsem, xssem, xmsem, xrsem,
+           ssem, rasem, rbsem, bssem, brasem, xssem, xmsem, xrsem,
            fsem, frsem, bfsem, bfrsem, ysem, yrsem):
     s = lax.axis_index("section")
     z = lax.axis_index("gy")
@@ -240,9 +240,19 @@
         k = 13 * core + t
         ab = k // 3
         c = k % 3
-        a, b = ab // 3, ab % 3
-        win = jnp.concatenate([window(gs, c, a, b), window(pgs, c, a, b)], axis=0)
-        part[pl.ds(pl.multiple_of(t * 320, 64), 320), :] = jnp.dot(unit_t[...], win, preferred_element_type=F32)
+        b = ab % 3
+        rows = pl.ds(pl.multiple_of((2 - b) * 16, 16), 128)
+        out = pl.ds(pl.multiple_of(t * 320, 64), 320)
+        for a in range(3):
+            f0, n = max(0, a - 1), 4 - abs(a - 1)
+
+            @pl.when(ab // 3 == a)
+            def _(a=a, f0=f0, n=n):
+                wins = [ref[c, pl.ds(f0 + 2 - a, n), rows, :].reshape(n * 128, 320) for ref in (gs, pgs)]
+                units = [unit_t[:, 512 * i + 128 * f0:512 * i + 128 * (f0 + n)] for i in range(2)]
+                part[out, :] = jnp.dot(
+                    jnp.concatenate(units, axis=1), jnp.concatenate(wins, axis=0), preferred_element_type=F32)
+
         return carry
 
     lax.fori_loop(0, 14, taps, 0)
@@ -302,10 +312,29 @@
 
         lax.fori_loop(0, 4, one, 0)
 
-    def chain_b(tau):
+    def straight(j):
+        return pltpu.make_async_remote_copy(
+            src_ref=bs.at[j], dst_ref=bra.at[z], send_sem=bssem.at[j], recv_sem=brasem.at[z],
+            device_id={"gy": 4 * core + j}, device_id_type=MESH)
+
+    def straight_sends():
         for j in range(4):
-            relay(j, tau, 4 - j % 2, bown.at[j], bs.at[j], bra.at[j], brb.at[j],
-                  bssem.at[j], brasem.at[j], brbsem.at[j], bfin)
+            @pl.when(4 * core + j != z)
+            def _(j=j):
+                bs[j] = bown[j].astype(BF16)
+                straight(j).start()
+
+    def straight_sum():
+        @pl.when(core == z // 4)
+        def _():
+            tot = bown[z - 4 * core]
+            for d in range(1, 8):
+                frm = (z + d) % 8
+                pltpu.make_async_remote_copy(
+                    src_ref=bs.at[0], dst_ref=bra.at[frm], send_sem=bssem.at[0], recv_sem=brasem.at[frm],
+                    device_id={"gy": frm}, device_id_type=MESH).wait_recv()
+                tot = tot + bra[frm].astype(F32)
+            bfin[...] = tot
 
     def ring(j, e, dst, rsem):
         plus = e == 1 or (e == 2 and j % 2 == 0)
@@ -345,8 +374,8 @@
             root_in(j, 3).wait_recv()
             bown[j] = odd(j, 0) + xr[j, 0].astype(F32) + xr[j, 1].astype(F32)
 
+    ring_0()
     chain_a(0)
-    ring_0()
 
     wcopy.wait()
 
@@ -361,7 +390,11 @@
         return carry
 
     acc[...] = jnp.zeros((512, 320), F32)
-    lax.fori_loop(0, 9, side, 0)
+    lax.fori_loop(0, 4, side, 0)
+    chain_a(1)
+    lax.fori_loop(4, 7, side, 0)
+    ring_1()
+    lax.fori_loop(7, 9, side, 0)
 
     def grad_body(i, carry):
         p0, p1 = carry
@@ -376,13 +409,12 @@
     pa_x[1:2, :] = jnp.sum(p1, axis=0, keepdims=True)
     gather(pa_x, rx_px, pxs, pxr, "gx", me)
 
-    ring_1()
-    chain_a(1)
+    chain_a(2)
     pa_z[...] = gathered(pa_x, rx_px, pxs, pxr, "gx", me)
     gather(pa_z, rx_pz, pzs, pzr, "gy", z)
+    chain_a(3)
     ring_2()
-    chain_b(0)
-    chain_a(2)
+    straight_sends()
 
     ptot = gathered(pa_z, rx_pz, pzs, pzr, "gy", z)
     par_ref[...] = ptot[0:3, :]
@@ -403,9 +435,6 @@
         device_id={"section": jnp.maximum(s - 1, 0)}, device_id_type=MESH)
     pl.when(s > 0)(lambda: ycopy.start())
 
-    chain_b(1)
-    chain_a(3)
-    chain_b(2)
     chain_a(4)
 
     root = z // 4
@@ -431,8 +460,7 @@
             def _():
                 frecv[pl.ds(xc, 1)] = fsend[pl.ds(xc, 1)]
 
-    chain_b(3)
-    chain_b(4)
+    straight_sum()
 
     @pl.when((root == 0) & (core == 0))
     def _():
@@ -476,13 +504,12 @@
                 pltpu.make_async_remote_copy(
                     src_ref=sbuf.at[j, i], dst_ref=ra.at[j, i], send_sem=ssem.at[j, i],
                     recv_sem=rasem.at[j, i], device_id={"gy": (z + 1) % 8}, device_id_type=MESH).wait_send()
-            pltpu.make_async_remote_copy(
-                src_ref=bs.at[j], dst_ref=bra.at[j], send_sem=bssem.at[j],
-                recv_sem=brasem.at[j], device_id={"gy": (z + 1) % 8}, device_id_type=MESH).wait_send()
 
         return carry
 
     lax.fori_loop(0, 4, drain, 0)
+    for j in range(4):
+        pl.when(4 * core + j != z)(lambda j=j: straight(j).wait_send())
     for j in range(4):
         long_in(j).wait_send()
         root_in(j, 1).wait_send()
@@ -497,6 +524,12 @@
     @pl.when(s == 3)
     def _():
         up_ref[...] = jnp.zeros((512, 320), BF16)
+
+
+def finish(up_in, dw_in, par_in, up_ref, dw_ref, par_ref):
+    up_ref[...] = up_in[...]
+    dw_ref[...] = dw_in[...].reshape(135, 1, 320)
+    par_ref[...] = par_in[...].reshape(3, 1, 320)
 
 
 def local(level_input, out_grad, conv_weight, norm_gain, norm_shift):
@@ -505,11 +538,7 @@
     V = pltpu.VMEM
     up, dw, par = pl.pallas_call(
         kernel,
-        out_shape=(
-            jax.ShapeDtypeStruct((512, 320), BF16),
-            jax.ShapeDtypeStruct((135, 320), F32),
-            jax.ShapeDtypeStruct((3, 320), F32),
-        ),
+        out_shape=(V((512, 320), BF16), V((135, 320), F32), V((3, 320), F32)),
         in_specs=[vm, vm, pl.BlockSpec(memory_space=pl.ANY), vm, vm],
         out_specs=(vm, vm, vm),
         scratch_shapes=[
@@ -521,13 +550,13 @@
             V((512, 320), BF16), V((512, 320), BF16), V((320, 1024), BF16),
             V((512, 320), F32), V((512, 320), F32), V((512, 320), F32), V((14 * 320 + 8, 320), F32), V((4, 8, 176, 256), F32),
             V((4, 4, 176, 256), BF16), V((4, 4, 176, 256), BF16), V((4, 4, 176, 256), BF16),
-            V((4, 176, 256), F32), V((4, 176, 256), F32), V((4, 176, 256), F32), V((4, 176, 256), F32),
+            V((4, 176, 256), F32), V((4, 176, 256), BF16), V((8, 176, 256), BF16),
             V((4, 3, 176, 256), BF16), V((4, 176, 256), BF16), V((4, 2, 176, 256), BF16),
             V((4, 176, 256), F32), V((4, 176, 256), F32), V((176, 256), F32), V((176, 256), F32),
             V((512, 320), BF16), V((512, 320), BF16),
             dma(()), dma((2,)), dma((2,)), dma((2,)), dma((2,)), dma(()), dma(()), dma(()), dma(()),
             dma((8,)), dma((8,)), dma((8,)), dma((8,)), dma((8,)), dma((8,)), dma((8,)), dma((8,)),
-            dma((4, 4)), dma((4, 4)), dma((4, 4)), dma((4,)), dma((4,)), dma((4,)), dma((4, 3)), dma((4,)), dma((4, 2)),
+            dma((4, 4)), dma((4, 4)), dma((4, 4)), dma((4,)), dma((8,)), dma((4, 3)), dma((4,)), dma((4, 2)),
             dma((4,)), dma((4,)), dma(()), dma(()), dma(()), dma(()),
         ],
         compiler_params=pltpu.CompilerParams(
@@ -537,7 +566,18 @@
         level_input.reshape(512, 320), out_grad.reshape(4, 128, 320), conv_weight.reshape(27, 320, 320),
         norm_gain, norm_shift,
     )
-    return up.reshape(1, 4, 8, 16, 320), dw[None], par[None]
+    up, dw, par = pl.pallas_call(
+        finish,
+        out_shape=(
+            jax.ShapeDtypeStruct((512, 320), BF16),
+            jax.ShapeDtypeStruct((135, 1, 320), F32),
+            jax.ShapeDtypeStruct((3, 1, 320), F32),
+        ),
+        in_specs=[vm, vm, vm],
+        out_specs=(vm, vm, vm),
+        compiler_params=pltpu.CompilerParams(vmem_limit_bytes=8 * 1024 * 1024),
+    )(*(pltpu.with_memory_space_constraint(v, pltpu.VMEM) for v in (up, dw, par)))
+    return up.reshape(1, 4, 8, 16, 320), dw.reshape(1, 135, 320), par.reshape(1, 3, 320)
 
 
 def solution(mesh):

time: 77.3 us -> 67.4 us (0.87); the launches traced: 76 us -> 67.3 us
  local copies, waits for them, and re-layouts: 4.89 us -> 0 us
  Pallas kernels: 70.5 us -> 66.7 us
    unnamed x3 -> x0, local copies, waits for them, and re-layouts: 4.89 us -> none
    pallas_call x1 -> x2, Pallas kernels: 70.5 us -> 66.7 us  [the longest x1 65.8 us: local(): pl.pallas_call(kernel, out_shape=(V((512, 320), BF16), V((135, 320), F32)...]
where the time goes in v3:
time: 67.4 us; the launch traced here: 67.3 us
  Pallas kernels  66.7 us (99%)
    pallas_call x1, Pallas kernels, local(): pl.pallas_call(kernel, out_shape=(V((512, 320), BF16), V((135, 320), F32)...  65.8 us

profile of v3, /device:TPU:8, one launch (start us, length us, event | category | flops | bytes accessed | tf_op | source)
XLA Modules:
  0.0 67.3 jit_solution(13401641099890616844)
XLA Ops:
  0.6 65.8 %shard_map.76 = (bf16[512,320]{1,0:T(8,128)(2,1)S(1)}, f32[135,320]{1,0:T(8,128)S(1)}, f32[3,320]{1,0:T(4,128)S(1)}) custom-call(bf16[512,320]{1,0:T(8,128)(2,1)} %bitcast.7, bf16[4,128,320]{2,1,0:T(8,128)(2,1)} %bitcast.8, bf16[27,320,320]{2,1,0:T(8,128)(2,1)} %bitcast.6, f32[1,320]{1,0:T(1,128)} %gain_ref.1, f32[1,320]{1,0:T(1,128)} %shift_ref.1), custom_call_target="tpu_custom_call" | custom-call | tf_op jit(solution)/shard_map/pallas_call | solution.py:539
  66.4 0.9 %shard_map.77 = (bf16[512,320]{1,0:T(8,128)(2,1)}, f32[135,1,320]{2,1,0:T(1,128)}, f32[3,1,320]{2,1,0:T(1,128)}) custom-call(bf16[512,320]{1,0:T(8,128)(2,1)S(1)} %get-tuple-element.9.up_in, f32[135,320]{1,0:T(8,128)S(1)} %get-tuple-element.10.dw_in, f32[3,320]{1,0:T(4,128)S(1)} %get-tuple-element.11.par_in), custom_call_target="tpu_custom_call" | custom-call | tf_op jit(solution)/shard_map/pallas_call | solution.py:569

commit v4 on v3

--- a/solution.py
+++ b/solution.py
@@ -29,11 +29,11 @@
 
 def kernel(x_ref, g_ref, w_hbm, gain_ref, shift_ref,
            up_ref, dw_ref, par_ref,
-           wbuf, gs, pgs, gf, tmp, edge_out, edge_l, edge_r,
+           wbuf, gs, pgs, gf, tmp, edge_out, edge_l, edge_r, corner_out, corner_in,
            st_x, rx_sx, st_z, rx_sz, pa_x, rx_px, pa_z, rx_pz,
            unit_own, unit_par, unit_t, acc, normed_b, slope_b, part, own,
            sbuf, ra, rb, bown, bs, bra, xs, xm, xr, fsend, frecv, bfin, brecv, lsend, lrecv,
-           wsem, zsem, zrsem, esem, ersem, gsem, grsem, usem, ursem,
+           wsem, zsem, zrsem, esem, ersem, csem, crsem, gsem, grsem, usem, ursem,
            sxs, sxr, szs, szr, pxs, pxr, pzs, pzr,
            ssem, rasem, rbsem, bssem, brasem, xssem, xmsem, xrsem,
            fsem, frsem, bfsem, bfrsem, ysem, yrsem):
@@ -60,6 +60,14 @@
     def _():
         pl.semaphore_signal(barrier, inc=1, device_id={"section": s + 1}, device_id_type=MESH)
 
+    for side in range(2):
+        for vert in range(2):
+            nx, nz = me + 2 * side - 1, z + 2 * vert - 1
+
+            @pl.when((nx >= 0) & (nx < 8) & (nz >= 0) & (nz < 8))
+            def _(nx=nx, nz=nz):
+                pl.semaphore_signal(barrier, inc=1, device_id={"gx": nx, "gy": nz}, device_id_type=MESH)
+
     def stat_body(i, carry):
         a, b = carry
         v = x_ref[pl.ds(pl.multiple_of(i * 64, 64), 64), :].astype(F32)
@@ -71,8 +79,71 @@
     st_x[0:1, :] = jnp.sum(a, axis=0, keepdims=True)
     st_x[1:2, :] = jnp.sum(b, axis=0, keepdims=True)
 
-    first_entry = 14 + jnp.where(s > 0, 1, 0) + jnp.where(s < 3, 1, 0)
-    pl.semaphore_wait(barrier, first_entry)
+    zrow = jnp.zeros((4, 16, 320), BF16)
+    part[14 * 320:14 * 320 + 8, :] = zero8
+    for c in range(3):
+        pgs[c, 0] = jnp.zeros((160, 320), BF16)
+        pgs[c, 5] = jnp.zeros((160, 320), BF16)
+        gs[c, 0] = jnp.zeros((160, 320), BF16)
+        gs[c, 5] = jnp.zeros((160, 320), BF16)
+
+    @pl.when(z == 0)
+    def _():
+        gs[1, 1:5, 0:16, :] = zrow
+
+    @pl.when(z == 7)
+    def _():
+        gs[1, 1:5, 144:160, :] = zrow
+
+    @pl.when(me == 0)
+    def _():
+        edge_l[...] = jnp.zeros((4, 3, 8, 128), F32)
+
+    @pl.when(me == 7)
+    def _():
+        edge_r[...] = jnp.zeros((4, 3, 8, 128), F32)
+
+    def lanes(v, l):
+        if l < 2:
+            return v[:, 128 * l:128 * l + 128]
+        return jnp.concatenate([v[:, 256:320], jnp.zeros((v.shape[0], 64), F32)], axis=1)
+
+    bsum = jnp.zeros((1, 320), F32)
+    corner_out[...] = jnp.zeros((2, 2, 3, 8, 128), F32)
+    for f in range(4):
+        v = g_ref[f]
+        gs[1, 1 + f, 16:144, :] = v
+        v = v.astype(F32)
+        bsum = bsum + jnp.sum(v, axis=0, keepdims=True)
+        for l in range(3):
+            gf[f, l] = lanes(v, l)
+            for side in range(2):
+                edge_out[side, f, l] = gf[f, l, pl.ds(15 * side, 8, stride=16), :]
+                corner_out[side, 0, l, f:f + 1, :] = gf[f, l, 15 * side:15 * side + 1, :]
+                corner_out[side, 1, l, f:f + 1, :] = gf[f, l, 112 + 15 * side:113 + 15 * side, :]
+    pa_x[...] = zero8
+    pa_x[2:3, :] = bsum
+
+    def corner(side, vert):
+        nx, nz = me + 2 * side - 1, z + 2 * vert - 1
+        fx, fz = me - 2 * side + 1, z - 2 * vert + 1
+        sent = (nx >= 0) & (nx < 8) & (nz >= 0) & (nz < 8)
+        due = (fx >= 0) & (fx < 8) & (fz >= 0) & (fz < 8)
+        copy = pltpu.make_async_remote_copy(
+            src_ref=corner_out.at[side, vert], dst_ref=corner_in.at[side, vert],
+            send_sem=csem.at[side, vert], recv_sem=crsem.at[side, vert],
+            device_id={"gx": jnp.clip(nx, 0, 7), "gy": jnp.clip(nz, 0, 7)}, device_id_type=MESH)
+        return sent, due, copy
+
+    corners = [corner(side, vert) for side in range(2) for vert in range(2)]
+    for q in range(4):
+        @pl.when(jnp.logical_not(corners[q][1]))
+        def _(q=q):
+            corner_in[q // 2, q % 2] = jnp.zeros((3, 8, 128), F32)
+
+    wide = jnp.where(me > 0, 1, 0) + jnp.where(me < 7, 1, 0)
+    tall = jnp.where(z > 0, 1, 0) + jnp.where(z < 7, 1, 0)
+    pl.semaphore_wait(barrier, 14 + jnp.where(s > 0, 1, 0) + jnp.where(s < 3, 1, 0) + wide * tall)
 
     def gather(src, dst, ssems, rsems, axis, at):
         out = []
@@ -103,58 +174,11 @@
             dst_ref=gs.at[1, pl.ds(1, 4), pl.ds(dst_row, 16), :],
             send_sem=zsem.at[i], recv_sem=zrsem.at[i], device_id={"gy": to}, device_id_type=MESH)
 
+    gather(st_x, rx_sx, sxs, sxr, "gx", me)
     up_halo = halo(0, 144, jnp.maximum(z - 1, 0), 0)
     down_halo = halo(112, 0, jnp.minimum(z + 1, 7), 1)
     pl.when(z > 0)(lambda: up_halo.start())
     pl.when(z < 7)(lambda: down_halo.start())
-    gather(st_x, rx_sx, sxs, sxr, "gx", me)
-
-    zrow = jnp.zeros((4, 16, 320), BF16)
-    part[14 * 320:14 * 320 + 8, :] = zero8
-    for c in range(3):
-        pgs[c, 0] = jnp.zeros((160, 320), BF16)
-        pgs[c, 5] = jnp.zeros((160, 320), BF16)
-        gs[c, 0] = jnp.zeros((160, 320), BF16)
-        gs[c, 5] = jnp.zeros((160, 320), BF16)
-
-    @pl.when(z == 0)
-    def _():
-        gs[1, 1:5, 0:16, :] = zrow
-
-    @pl.when(z == 7)
-    def _():
-        gs[1, 1:5, 144:160, :] = zrow
-
-    bsum = jnp.zeros((1, 320), F32)
-    for f in range(4):
-        v = g_ref[f]
-        gs[1, 1 + f, 16:144, :] = v
-        v = v.astype(F32)
-        bsum = bsum + jnp.sum(v, axis=0, keepdims=True)
-    pa_x[...] = zero8
-    pa_x[2:3, :] = bsum
-
-    @pl.when(z > 0)
-    def _():
-        up_halo.wait_send()
-        down_halo.wait_recv()
-
-    @pl.when(z < 7)
-    def _():
-        down_halo.wait_send()
-        up_halo.wait_recv()
-
-    for f in range(4):
-        v = gs[1, 1 + f].astype(F32)
-        gf[f, 0] = v[:, 0:128]
-        gf[f, 1] = v[:, 128:256]
-        gf[f, 2] = jnp.concatenate([v[:, 256:320], jnp.zeros((160, 64), F32)], axis=1)
-    for f in range(4):
-        for l in range(3):
-            edge_out[0, f, l] = jnp.zeros((16, 128), F32)
-            edge_out[1, f, l] = jnp.zeros((16, 128), F32)
-            edge_out[0, f, l, 0:10, :] = gf[f, l, pl.ds(0, 10, stride=16), :]
-            edge_out[1, f, l, 0:10, :] = gf[f, l, pl.ds(15, 10, stride=16), :]
     to_left = pltpu.make_async_remote_copy(
         src_ref=edge_out.at[0], dst_ref=edge_r, send_sem=esem.at[0], recv_sem=ersem.at[0],
         device_id={"gx": jnp.maximum(me - 1, 0)}, device_id_type=MESH)
@@ -163,18 +187,22 @@
         device_id={"gx": jnp.minimum(me + 1, 7)}, device_id_type=MESH)
     pl.when(me > 0)(lambda: to_left.start())
     pl.when(me < 7)(lambda: to_right.start())
-
-    @pl.when(me == 0)
-    def _():
-        edge_l[...] = jnp.zeros((4, 3, 16, 128), F32)
-
-    @pl.when(me == 7)
-    def _():
-        edge_r[...] = jnp.zeros((4, 3, 16, 128), F32)
+    for sent, _, copy in corners:
+        pl.when(sent)(lambda copy=copy: copy.start())
 
     st_z[...] = gathered(st_x, rx_sx, sxs, sxr, "gx", me)
     gather(st_z, rx_sz, szs, szr, "gy", z)
 
+    @pl.when(z > 0)
+    def _():
+        up_halo.wait_send()
+        down_halo.wait_recv()
+
+    @pl.when(z < 7)
+    def _():
+        down_halo.wait_send()
+        up_halo.wait_recv()
+
     @pl.when(me > 0)
     def _():
         to_left.wait_send()
@@ -185,14 +213,23 @@
         to_right.wait_send()
         to_left.wait_recv()
 
+    for sent, due, copy in corners:
+        pl.when(sent)(lambda copy=copy: copy.wait_send())
+        pl.when(due)(lambda copy=copy: copy.wait_recv())
+
     for f in range(4):
+        ext = gs[1, 1 + f].astype(F32)
         for l in range(3):
             w = 128 if l < 2 else 64
-            v = gf[f, l]
+            v = lanes(ext, l)
             tmp[0] = pltpu.roll(v, 1, 0)
             tmp[1] = pltpu.roll(v, 159, 0)
-            tmp[0, pl.ds(0, 10, stride=16), :] = edge_l[f, l, 0:10, :]
-            tmp[1, pl.ds(15, 10, stride=16), :] = edge_r[f, l, 0:10, :]
+            tmp[0, pl.ds(16, 8, stride=16), :] = edge_l[f, l]
+            tmp[1, pl.ds(31, 8, stride=16), :] = edge_r[f, l]
+            tmp[0, 0:1, :] = corner_in[1, 1, l, f:f + 1, :]
+            tmp[0, 144:145, :] = corner_in[1, 0, l, f:f + 1, :]
+            tmp[1, 15:16, :] = corner_in[0, 1, l, f:f + 1, :]
+            tmp[1, 159:160, :] = corner_in[0, 0, l, f:f + 1, :]
             gs[2, 1 + f, :, 128 * l:128 * l + w] = tmp[0, :, 0:w].astype(BF16)
             gs[0, 1 + f, :, 128 * l:128 * l + w] = tmp[1, :, 0:w].astype(BF16)
     swap = pltpu.make_async_remote_copy(
@@ -204,6 +241,22 @@
         v = ref[c, pl.ds(2 - a, 4), pl.ds(pl.multiple_of((2 - b) * 16, 16), 128), :]
         return v.reshape(512, 320)
 
+    def side(ab, carry):
+        a, b = ab // 3, ab % 3
+        tot = None
+        for c in range(3):
+            wk = wbuf[ab * 3 + c]
+            d = lax.dot_general(window(gs, c, a, b), wk, (((1,), (1,)), ((), ())), preferred_element_type=F32)
+            tot = d if tot is None else tot + d
+        acc[...] += tot
+        return carry
+
+    def sides(lo, hi):
+        lax.fori_loop(lo, hi, side, 0)
+
+    acc[...] = jnp.zeros((512, 320), F32)
+    wcopy.wait()
+    sides(0, 2)
     ia = jnp.floor((lax.broadcasted_iota(jnp.int32, (320, 320), 0).astype(F32) + 0.5) * 0.1)
     ib = jnp.floor((lax.broadcasted_iota(jnp.int32, (320, 320), 1).astype(F32) + 0.5) * 0.1)
     grp = jnp.where(ia == ib, 1.0, 0.0).astype(F32)
@@ -232,11 +285,13 @@
         device_id={"gx": partner}, device_id_type=MESH)
     swap_u.start()
     unit_t[:, 0:512] = unit_own[...].T
+    sides(2, 4)
     swap.wait()
     swap_u.wait()
     unit_t[:, 512:1024] = unit_par[...].T
 
-    def taps(t, carry):
+    def taps(u, carry):
+        t = jnp.where((4 * core - z + 9) % 8 < 4, 13 - u, u)
         k = 13 * core + t
         ab = k // 3
         c = k % 3
@@ -255,7 +310,6 @@
 
         return carry
 
-    lax.fori_loop(0, 14, taps, 0)
 
     def packing(j, carry):
         for d in range(8):
@@ -265,8 +319,6 @@
             own[j, d, 0:136, :] = main
             own[j, d, 136:176, :] = rest
         return carry
-
-    lax.fori_loop(0, 4, packing, 0)
 
     def relay(j, tau, top, mine, sb, up_in, down_in, s_send, s_up, s_down, result):
         delta = (4 * core + j - z + 8) % 8
@@ -303,11 +355,14 @@
                 sends_down().wait_recv()
                 result[...] = mine[...] + up_in[...].astype(F32) + down_in[...].astype(F32)
 
+    def slab_a(j, tau):
+        for i in range(4):
+            relay(j, tau, 4 - i % 2, own.at[j, 2 * i], sbuf.at[j, i], ra.at[j, i], rb.at[j, i],
+                  ssem.at[j, i], rasem.at[j, i], rbsem.at[j, i], fsend.at[i])
+
     def chain_a(tau):
         def one(j, carry):
-            for i in range(4):
-                relay(j, tau, 4 - i % 2, own.at[j, 2 * i], sbuf.at[j, i], ra.at[j, i], rb.at[j, i],
-                      ssem.at[j, i], rasem.at[j, i], rbsem.at[j, i], fsend.at[i])
+            slab_a(j, tau)
             return carry
 
         lax.fori_loop(0, 4, one, 0)
@@ -352,14 +407,12 @@
     def root_in(j, e):
         return ring(j, e, xr.at[j, e // 2], xrsem.at[j, e // 2])
 
-    def ring_0():
-        for j in range(4):
-            xs[j, 1] = odd(j, 2).astype(BF16)
-            long_in(j).start()
-        for j in range(4):
-            e = 3 if j % 2 == 0 else 1
-            xs[j, e - 1] = odd(j, e).astype(BF16)
-            root_in(j, e).start()
+    def ring_0(j):
+        xs[j, 1] = odd(j, 2).astype(BF16)
+        long_in(j).start()
+        e = 3 if j % 2 == 0 else 1
+        xs[j, e - 1] = odd(j, e).astype(BF16)
+        root_in(j, e).start()
 
     def ring_1():
         for j in range(4):
@@ -374,27 +427,14 @@
             root_in(j, 3).wait_recv()
             bown[j] = odd(j, 0) + xr[j, 0].astype(F32) + xr[j, 1].astype(F32)
 
-    ring_0()
-    chain_a(0)
-
-    wcopy.wait()
-
-    def side(ab, carry):
-        a, b = ab // 3, ab % 3
-        tot = None
-        for c in range(3):
-            wk = wbuf[ab * 3 + c]
-            d = lax.dot_general(window(gs, c, a, b), wk, (((1,), (1,)), ((), ())), preferred_element_type=F32)
-            tot = d if tot is None else tot + d
-        acc[...] += tot
-        return carry
-
-    acc[...] = jnp.zeros((512, 320), F32)
-    lax.fori_loop(0, 4, side, 0)
-    chain_a(1)
-    lax.fori_loop(4, 7, side, 0)
-    ring_1()
-    lax.fori_loop(7, 9, side, 0)
+    late = (4 * core - z + 9) % 8 < 4
+    for i, (t0, t1) in enumerate(((0, 4), (4, 8), (8, 11), (11, 14))):
+        lax.fori_loop(t0, t1, taps, 0)
+        jd = jnp.where(late, 3 - i, i)
+        packing(jd, 0)
+        slab_a(jd, 0)
+        pl.when(late)(lambda i=i: ring_0(3 - i))
+        pl.when(jnp.logical_not(late))(lambda i=i: ring_0(i))
 
     def grad_body(i, carry):
         p0, p1 = carry
@@ -404,11 +444,14 @@
         return (p0 + jnp.sum((ag * normed_b[rows, :]).reshape(8, 8, 320), axis=0),
                 p1 + jnp.sum(ag.reshape(8, 8, 320), axis=0))
 
+    chain_a(1)
+    sides(4, 7)
+    ring_1()
+    sides(7, 9)
     p0, p1 = lax.fori_loop(0, 8, grad_body, (zero8, zero8))
     pa_x[0:1, :] = jnp.sum(p0, axis=0, keepdims=True)
     pa_x[1:2, :] = jnp.sum(p1, axis=0, keepdims=True)
     gather(pa_x, rx_px, pxs, pxr, "gx", me)
-
     chain_a(2)
     pa_z[...] = gathered(pa_x, rx_px, pxs, pxr, "gx", me)
     gather(pa_z, rx_pz, pzs, pzr, "gy", z)
@@ -543,8 +586,9 @@
         out_specs=(vm, vm, vm),
         scratch_shapes=[
             V((27, 320, 320), BF16), V((3, 6, 160, 320), BF16), V((3, 6, 160, 320), BF16),
-            V((4, 3, 160, 128), F32), V((2, 160, 128), F32),
-            V((2, 4, 3, 16, 128), F32), V((4, 3, 16, 128), F32), V((4, 3, 16, 128), F32),
+            V((4, 3, 128, 128), F32), V((2, 160, 128), F32),
+            V((2, 4, 3, 8, 128), F32), V((4, 3, 8, 128), F32), V((4, 3, 8, 128), F32),
+            V((2, 2, 3, 8, 128), F32), V((2, 2, 3, 8, 128), F32),
             V((8, 320), F32), V((8, 8, 320), F32), V((8, 320), F32), V((8, 8, 320), F32),
             V((8, 320), F32), V((8, 8, 320), F32), V((8, 320), F32), V((8, 8, 320), F32),
             V((512, 320), BF16), V((512, 320), BF16), V((320, 1024), BF16),
@@ -554,7 +598,7 @@
             V((4, 3, 176, 256), BF16), V((4, 176, 256), BF16), V((4, 2, 176, 256), BF16),
             V((4, 176, 256), F32), V((4, 176, 256), F32), V((176, 256), F32), V((176, 256), F32),
             V((512, 320), BF16), V((512, 320), BF16),
-            dma(()), dma((2,)), dma((2,)), dma((2,)), dma((2,)), dma(()), dma(()), dma(()), dma(()),
+            dma(()), dma((2,)), dma((2,)), dma((2,)), dma((2,)), dma((2, 2)), dma((2, 2)), dma(()), dma(()), dma(()), dma(()),
             dma((8,)), dma((8,)), dma((8,)), dma((8,)), dma((8,)), dma((8,)), dma((8,)), dma((8,)),
             dma((4, 4)), dma((4, 4)), dma((4, 4)), dma((4,)), dma((8,)), dma((4, 3)), dma((4,)), dma((4, 2)),
             dma((4,)), dma((4,)), dma(()), dma(()), dma(()), dma(()),

time: 67.4 us -> 63.4 us (0.941)
  Pallas kernels: 66.7 us -> 62.1 us
    pallas_call x1, Pallas kernels: 65.8 us -> 61.2 us  [local(): pl.pallas_call(kernel, out_shape=(V((512, 320), BF16), V((135, 320), F32)...]
where the time goes in v4:
time: 63.4 us; the launch traced here: 62.7 us
  Pallas kernels  62.1 us (98%)
  between operations  0.64 us (1%)
    pallas_call x1, Pallas kernels, local(): pl.pallas_call(kernel, out_shape=(V((512, 320), BF16), V((135, 320), F32)...  61.2 us

profile of v4, /device:TPU:8, one launch (start us, length us, event | category | flops | bytes accessed | tf_op | source)
XLA Modules:
  0.0 62.7 jit_solution(5245581106861044373)
XLA Ops:
  0.6 61.2 %shard_map.76 = (bf16[512,320]{1,0:T(8,128)(2,1)S(1)}, f32[135,320]{1,0:T(8,128)S(1)}, f32[3,320]{1,0:T(4,128)S(1)}) custom-call(bf16[512,320]{1,0:T(8,128)(2,1)} %bitcast.7, bf16[4,128,320]{2,1,0:T(8,128)(2,1)} %bitcast.8, bf16[27,320,320]{2,1,0:T(8,128)(2,1)} %bitcast.6, f32[1,320]{1,0:T(1,128)} %gain_ref.1, f32[1,320]{1,0:T(1,128)} %shift_ref.1), custom_call_target="tpu_custom_call" | custom-call | tf_op jit(solution)/shard_map/pallas_call | solution.py:582
  61.8 0.9 %shard_map.77 = (bf16[512,320]{1,0:T(8,128)(2,1)}, f32[135,1,320]{2,1,0:T(1,128)}, f32[3,1,320]{2,1,0:T(1,128)}) custom-call(bf16[512,320]{1,0:T(8,128)(2,1)S(1)} %get-tuple-element.9.up_in, f32[135,320]{1,0:T(8,128)S(1)} %get-tuple-element.10.dw_in, f32[3,320]{1,0:T(4,128)S(1)} %get-tuple-element.11.par_in), custom_call_target="tpu_custom_call" | custom-call | tf_op jit(solution)/shard_map/pallas_call | solution.py:613

commit v5 on v4

--- a/solution.py
+++ b/solution.py
@@ -242,13 +242,21 @@
         return v.reshape(512, 320)
 
     def side(ab, carry):
-        a, b = ab // 3, ab % 3
-        tot = None
-        for c in range(3):
-            wk = wbuf[ab * 3 + c]
-            d = lax.dot_general(window(gs, c, a, b), wk, (((1,), (1,)), ((), ())), preferred_element_type=F32)
-            tot = d if tot is None else tot + d
-        acc[...] += tot
+        b = ab % 3
+        rows = pl.ds(pl.multiple_of((2 - b) * 16, 16), 128)
+        for a in range(3):
+            f0, n = max(0, a - 1), 4 - abs(a - 1)
+
+            @pl.when(ab // 3 == a)
+            def _(a=a, f0=f0, n=n):
+                tot = None
+                for c in range(3):
+                    win = gs[c, f0 + 2 - a:f0 + 2 - a + n, rows, :].reshape(n * 128, 320)
+                    d = lax.dot_general(
+                        win, wbuf[ab * 3 + c], (((1,), (1,)), ((), ())), preferred_element_type=F32)
+                    tot = d if tot is None else tot + d
+                acc[128 * f0:128 * (f0 + n), :] += tot
+
         return carry
 
     def sides(lo, hi):
@@ -256,7 +264,7 @@
 
     acc[...] = jnp.zeros((512, 320), F32)
     wcopy.wait()
-    sides(0, 2)
+    sides(0, 3)
     ia = jnp.floor((lax.broadcasted_iota(jnp.int32, (320, 320), 0).astype(F32) + 0.5) * 0.1)
     ib = jnp.floor((lax.broadcasted_iota(jnp.int32, (320, 320), 1).astype(F32) + 0.5) * 0.1)
     grp = jnp.where(ia == ib, 1.0, 0.0).astype(F32)
@@ -285,7 +293,7 @@
         device_id={"gx": partner}, device_id_type=MESH)
     swap_u.start()
     unit_t[:, 0:512] = unit_own[...].T
-    sides(2, 4)
+    sides(3, 6)
     swap.wait()
     swap_u.wait()
     unit_t[:, 512:1024] = unit_par[...].T
@@ -445,9 +453,9 @@
                 p1 + jnp.sum(ag.reshape(8, 8, 320), axis=0))
 
     chain_a(1)
-    sides(4, 7)
+    sides(6, 8)
     ring_1()
-    sides(7, 9)
+    sides(8, 9)
     p0, p1 = lax.fori_loop(0, 8, grad_body, (zero8, zero8))
     pa_x[0:1, :] = jnp.sum(p0, axis=0, keepdims=True)
     pa_x[1:2, :] = jnp.sum(p1, axis=0, keepdims=True)

time: 63.4 us -> 63 us (level)
  no operation moved by 1% of the time
where the time goes in v5:
time: 63 us; the launch traced here: 62.7 us
  Pallas kernels  62.1 us (99%)
  between operations  0.64 us (1%)
    pallas_call x1, Pallas kernels, local(): pl.pallas_call(kernel, out_shape=(V((512, 320), BF16), V((135, 320), F32)...  61.2 us

profile of v5, /device:TPU:8, one launch (start us, length us, event | category | flops | bytes accessed | tf_op | source)
XLA Modules:
  0.0 62.7 jit_solution(3196577185462526820)
XLA Ops:
  0.6 61.2 %shard_map.76 = (bf16[512,320]{1,0:T(8,128)(2,1)S(1)}, f32[135,320]{1,0:T(8,128)S(1)}, f32[3,320]{1,0:T(4,128)S(1)}) custom-call(bf16[512,320]{1,0:T(8,128)(2,1)} %bitcast.7, bf16[4,128,320]{2,1,0:T(8,128)(2,1)} %bitcast.8, bf16[27,320,320]{2,1,0:T(8,128)(2,1)} %bitcast.6, f32[1,320]{1,0:T(1,128)} %gain_ref.1, f32[1,320]{1,0:T(1,128)} %shift_ref.1), custom_call_target="tpu_custom_call" | custom-call | tf_op jit(solution)/shard_map/pallas_call | solution.py:590
  61.8 0.9 %shard_map.77 = (bf16[512,320]{1,0:T(8,128)(2,1)}, f32[135,1,320]{2,1,0:T(1,128)}, f32[3,1,320]{2,1,0:T(1,128)}) custom-call(bf16[512,320]{1,0:T(8,128)(2,1)S(1)} %get-tuple-element.9.up_in, f32[135,320]{1,0:T(8,128)S(1)} %get-tuple-element.10.dw_in, f32[3,320]{1,0:T(4,128)S(1)} %get-tuple-element.11.par_in), custom_call_target="tpu_custom_call" | custom-call | tf_op jit(solution)/shard_map/pallas_call | solution.py:621
